TPU v7x, 32 devices: a whole 2x2x4 slice. The times are simulated.
32 devices in a mesh: dom: 8 (over z, y), rep: 4 (over x, core).
Axes of the slice: x: 2, y: 2, z: 4, core: 2. Of those that a mesh axis runs over, the one named last changes fastest.
Arguments:
- ns_shape: bfloat16 [64, 256], replicated, may hold values from -0.75 to 0.75
- nm_shape: bfloat16 [64, 256], replicated, may hold values from -0.75 to 0.75
- sec_disp: bfloat16 [64, 262144], P(None, ('dom', 'rep')), may hold values from -6 to 6
- mst_disp: bfloat16 [64, 262144], P(None, ('dom', 'rep')), may hold values from -6 to 6
- gap_offset: float32 [262144], P(('dom', 'rep')), may hold values from -6 to 6
- quad_weight: float32 [256], replicated, may hold values from 0.25 to 4
- jacobian: float32 [262144], P(('dom', 'rep')), may hold values from 0.0005 to 0.005
- segment_slot: int32 [262144], P(('dom', 'rep')), may hold values from 0 to 1279, as said below
- face_id: int32 [262144], P(('dom', 'rep')), may hold values from 0 to 1073741823
- search_rank: int32 [262144], P(('dom', 'rep')), may hold values from 0 to 3
- live_rows: int32 [32], P(('dom', 'rep')), may hold values from 1024 to 8192, as said below
Outputs:
- contact_force: bfloat16 [64, 262144], P(None, ('dom', 'rep'))
- seg_pen: float32 [8192], P('dom')
- seg_face: int32 [8192], P('dom')
- seg_gap: float32 [8192], P('dom')
- mean_gap: float32 [], replicated
Inputs may be any that keep to these rules, and one draw needn't show every extreme that they name: `segment_slot`: A row's segment is (1024 times the dom index of its device plus its slot) modulo 8192; slots of 1024 or more reach the next dom index's first 256 segments. `live_rows`: entry b counts the live rows of the device with flat index b (dom-major); they are that device's first rows, the rest are padding; some device is full in every draw.
All inputs are finite; a program needn't handle non-finite values.
Results may differ from a plain program's by a relative error of at most 0.0055.
Values sent between devices are 32-bit elements; how exact they have to be, the bound alone decides.
No kernel may reach another device: no remote copies, remote signals or barrier semaphores. Data moves between devices by JAX's collectives and lax.ppermute only.
A program may use at most 64 MiB of HBM per device.

v0:
```python
import math

import jax
import jax.numpy as jnp
from jax import lax
from jax.sharding import PartitionSpec as P

SEG_DEV = 1024
SPILL = 256


PENALTY = 400.0
LOWEST_FILL = -1e30
FACE_LIMIT = 1073741824


def combined_all(value, axis, join):
    pieces = jax.tree.map(lambda part: lax.all_gather(part, axis), value)
    head = jax.tree.map(lambda part: part[0], pieces)
    tail = jax.tree.map(lambda part: part[1:], pieces)
    running, _ = lax.scan(lambda running, share: (join(running, share), None), head, tail)
    return running


def passed_along(x, axis, by):
    length = lax.axis_size(axis)
    return lax.ppermute(x, axis, [(i, (i + by) % length) for i in range(length)])


def project(shape_table, displace):
    return lax.dot_general(
        shape_table, displace, (((0,), (0,)), ((), ())), preferred_element_type=jnp.float32
    )


def combine(earlier, latter):
    prefer = (latter[1] > earlier[1]) | (latter[1] == earlier[1]) & (latter[2] < earlier[2])
    head = (
        jnp.maximum(earlier[0], latter[0]),
        jnp.where(prefer, latter[1], earlier[1]),
        jnp.where(prefer, latter[2], earlier[2]),
    )
    return head + tuple(
        (left_part + right_part for left_part, right_part in zip(earlier[3:], latter[3:]))
    )


def window_stats(gap_field, jac_row, weights, slots, faces, ranks, live, window_len):
    row_pen = jnp.max(-gap_field, axis=0)
    row_gap = jac_row * jnp.dot(weights, gap_field, precision=lax.Precision.HIGHEST)
    row_area = jac_row * jnp.sum(weights)
    row_count = gap_field.shape[1]
    block_len = math.gcd(row_count, 1024)
    turns = row_count // block_len
    slot_ids = jnp.arange(window_len, dtype=jnp.int32)[:, None]
    paired = jnp.stack([row_gap, row_area], axis=0)

    def one_block(turn, carry):
        begin = turn * block_len

        def take(values):
            return lax.dynamic_slice_in_dim(values, begin, block_len, values.ndim - 1)

        block_live = take(live)
        block_ranks = take(ranks)
        member = slot_ids == take(slots)[None, :]
        hit = member & block_live[None, :]
        penalty_max = jnp.max(jnp.where(hit, take(row_pen)[None, :], LOWEST_FILL), axis=1)
        best_rank = jnp.max(jnp.where(hit, block_ranks[None, :], -1), axis=1)
        row_best = jnp.max(jnp.where(member, best_rank[:, None], -1), axis=0)
        chosen = jnp.where(block_live & (block_ranks == row_best), take(faces), FACE_LIMIT)
        lowest_face = jnp.min(jnp.where(member, chosen[None, :], FACE_LIMIT), axis=1)
        sums = lax.dot_general(
            take(paired),
            hit.astype(jnp.float32),
            (((1,), (1,)), ((), ())),
            precision=lax.Precision.HIGHEST,
        )
        fresh = (penalty_max, best_rank, lowest_face, sums[0], sums[1])
        return combine(carry, fresh)

    start = (
        jnp.full((window_len,), LOWEST_FILL, jnp.float32),
        jnp.full((window_len,), -1, jnp.int32),
        jnp.full((window_len,), FACE_LIMIT, jnp.int32),
        jnp.zeros((window_len,), jnp.float32),
        jnp.zeros((window_len,), jnp.float32),
    )
    return lax.fori_loop(0, turns, one_block, start)


def shards(
    ns_shape,
    nm_shape,
    sec_disp,
    mst_disp,
    gap_offset,
    quad_weight,
    jacobian,
    segment_slot,
    face_id,
    search_rank,
    live_rows,
):
    row_count = sec_disp.shape[1]
    window_len = SEG_DEV + SPILL
    gap_field = project(ns_shape, sec_disp) - project(nm_shape, mst_disp) + gap_offset[None, :]
    live = jnp.arange(row_count, dtype=jnp.int32) < live_rows[0]
    load = jnp.where(
        live[None, :],
        quad_weight[:, None] * jacobian[None, :] * PENALTY * jnp.maximum(-gap_field, 0.0),
        0.0,
    ).astype(jnp.bfloat16)
    contact_force = jnp.dot(ns_shape, load, preferred_element_type=jnp.float32).astype(jnp.bfloat16)
    stats = window_stats(
        gap_field, jacobian, quad_weight, segment_slot, face_id, search_rank, live, window_len
    )
    grouped = combined_all(stats, "rep", combine)
    spill = tuple((part[SEG_DEV:] for part in grouped))
    arrived = passed_along(spill, "dom", 1)
    leading = combine(tuple((part[:SPILL] for part in grouped)), arrived)
    own = tuple(
        (
            jnp.concatenate([lead_part, part[SPILL:SEG_DEV]])
            for lead_part, part in zip(leading, grouped)
        )
    )
    seg_pen = jnp.where(own[1] < 0, jnp.float32(0.0), own[0])
    seg_face = jnp.where(own[1] < 0, -1, own[2]).astype(jnp.int32)
    seg_gap = own[3]
    gap_total, area_total = lax.psum((jnp.sum(own[3]), jnp.sum(own[4])), "dom")
    mean_gap = gap_total / area_total
    return (contact_force, seg_pen, seg_face, seg_gap, mean_gap)


def solution(mesh):
    return jax.shard_map(
        shards,
        mesh=mesh,
        in_specs=(
            P(),
            P(),
            P(None, ("dom", "rep")),
            P(None, ("dom", "rep")),
            P(("dom", "rep")),
            P(),
            P(("dom", "rep")),
            P(("dom", "rep")),
            P(("dom", "rep")),
            P(("dom", "rep")),
            P(("dom", "rep")),
        ),
        out_specs=(P(None, ("dom", "rep")), P("dom"), P("dom"), P("dom"), P()),
        check_vma=False,
    )
```

profile of v0, /device:TPU:0, one launch (start us, length us, event | category | flops | bytes accessed | tf_op | source)
XLA Modules:
  0.0 163.1 jit_solution(12261108922890064860)
XLA Ops:
  1.5 5.7 %fusion.28 = f32[256,8192]{1,0:T(8,128)} fusion(bf16[64,256]{1,0:T(8,128)(2,1)} %param.15, bf16[64,8192]{1,0:T(8,128)(2,1)} %param.17), kind=kOutput, calls=%fused_computation.69 | convolution fusion | flops 268435456 | bytes 9469952 | tf_op jit(solution)/shard_map/dot_general | solution.py:31
  7.8 4.8 %negate_reduce_fusion = (f32[8192]{0:T(1024)S(1)}, f32[256,8192]{1,0:T(8,128)S(1)}) fusion(f32[8192]{0:T(1024)S(1)} %copy-done.2, f32[256,8192]{1,0:T(8,128)} %fusion.28, bf16[64,256]{1,0:T(8,128)(2,1)S(1)} %copy-done.3, bf16[64,8192]{1,0:T(8,128)(2,1)S(1)} %copy-done), kind=kOutput, calls=%fused_computation.38 | convolution fusion | flops 276815872 | bytes 17924096 | tf_op jit(solution)/shard_map/dot_general | solution.py:31
  12.7 3.2 %copy-done.1 = f32[256,8192]{1,0:T(8,128)} copy-done((f32[256,8192]{1,0:T(8,128)}, f32[256,8192]{1,0:T(8,128)S(1)}, u32[]{:S(2)}) %copy-start.1) | copy-done | bytes 8388632
  15.9 4.4 %fusion.29 = f32[1,8192]{1,0:T(1,128)S(1)} fusion(f32[256,8192]{1,0:T(8,128)S(1)} %get-tuple-element.406, f32[256,1]{0,1:T(1,128)S(1)} %bitcast.38), kind=kOutput, calls=%fused_computation.70 | convolution fusion | flops 25165824 | bytes 8422400 | tf_op jit(solution)/shard_map/dot_general | solution.py:50
  21.0 70.1 %while.41 = (s32[]{:T(128)}, f32[1280]{0:T(1024)S(1)}, s32[1280]{0:T(1024)S(1)}, s32[1280]{0:T(1024)S(1)}, f32[1280]{0:T(1024)S(1)}, /*index=5*/f32[1280]{0:T(10...) while((s32[]{:T(128)}, f32[1280]{0:T(1024)S(1)}, ...), condition=%wide.region_7.8_spmd.clone, body=%wide.region_2.7_spmd.clone.sunk | while | flops 52446216 | bytes 220391 | solution.py:89
  21.9 2.5 %fusion.54 = f32[2,1280]{1,0:T(2,128)S(1)} fusion(s32[1024]{0:T(1024)S(1)} %dynamic_slice.94, pred[1024]{0:T(1024)(128)(4,1)S(1)} %dynamic_slice.95, f32[2,8192]{1,0:T(2,128)S(1)} %get-tuple-element.615, s32[]{:T(128)S(6)} %select_n.142), kind=kOutput, calls=%fused_computation.13.clone.1 | convolution fusion | flops 34078720 | bytes 23556 | tf_op jit(solution)/shard_map/while/body/eval_jaxpr/dot_general | solution.py:73
  30.7 2.5 %fusion.54 = f32[2,1280]{1,0:T(2,128)S(1)} fusion(s32[1024]{0:T(1024)S(1)} %dynamic_slice.94, pred[1024]{0:T(1024)(128)(4,1)S(1)} %dynamic_slice.95, f32[2,8192]{1,0:T(2,128)S(1)} %get-tuple-element.615, s32[]{:T(128)S(6)} %select_n.142), kind=kOutput, calls=%fused_computation.13.clone.1 | convolution fusion | flops 34078720 | bytes 23556 | tf_op jit(solution)/shard_map/while/body/eval_jaxpr/dot_general | solution.py:73
  39.4 2.5 %fusion.54 = f32[2,1280]{1,0:T(2,128)S(1)} fusion(s32[1024]{0:T(1024)S(1)} %dynamic_slice.94, pred[1024]{0:T(1024)(128)(4,1)S(1)} %dynamic_slice.95, f32[2,8192]{1,0:T(2,128)S(1)} %get-tuple-element.615, s32[]{:T(128)S(6)} %select_n.142), kind=kOutput, calls=%fused_computation.13.clone.1 | convolution fusion | flops 34078720 | bytes 23556 | tf_op jit(solution)/shard_map/while/body/eval_jaxpr/dot_general | solution.py:73
  48.2 2.5 %fusion.54 = f32[2,1280]{1,0:T(2,128)S(1)} fusion(s32[1024]{0:T(1024)S(1)} %dynamic_slice.94, pred[1024]{0:T(1024)(128)(4,1)S(1)} %dynamic_slice.95, f32[2,8192]{1,0:T(2,128)S(1)} %get-tuple-element.615, s32[]{:T(128)S(6)} %select_n.142), kind=kOutput, calls=%fused_computation.13.clone.1 | convolution fusion | flops 34078720 | bytes 23556 | tf_op jit(solution)/shard_map/while/body/eval_jaxpr/dot_general | solution.py:73
  56.9 2.5 %fusion.54 = f32[2,1280]{1,0:T(2,128)S(1)} fusion(s32[1024]{0:T(1024)S(1)} %dynamic_slice.94, pred[1024]{0:T(1024)(128)(4,1)S(1)} %dynamic_slice.95, f32[2,8192]{1,0:T(2,128)S(1)} %get-tuple-element.615, s32[]{:T(128)S(6)} %select_n.142), kind=kOutput, calls=%fused_computation.13.clone.1 | convolution fusion | flops 34078720 | bytes 23556 | tf_op jit(solution)/shard_map/while/body/eval_jaxpr/dot_general | solution.py:73
  65.6 2.5 %fusion.54 = f32[2,1280]{1,0:T(2,128)S(1)} fusion(s32[1024]{0:T(1024)S(1)} %dynamic_slice.94, pred[1024]{0:T(1024)(128)(4,1)S(1)} %dynamic_slice.95, f32[2,8192]{1,0:T(2,128)S(1)} %get-tuple-element.615, s32[]{:T(128)S(6)} %select_n.142), kind=kOutput, calls=%fused_computation.13.clone.1 | convolution fusion | flops 34078720 | bytes 23556 | tf_op jit(solution)/shard_map/while/body/eval_jaxpr/dot_general | solution.py:73
  74.4 2.5 %fusion.54 = f32[2,1280]{1,0:T(2,128)S(1)} fusion(s32[1024]{0:T(1024)S(1)} %dynamic_slice.94, pred[1024]{0:T(1024)(128)(4,1)S(1)} %dynamic_slice.95, f32[2,8192]{1,0:T(2,128)S(1)} %get-tuple-element.615, s32[]{:T(128)S(6)} %select_n.142), kind=kOutput, calls=%fused_computation.13.clone.1 | convolution fusion | flops 34078720 | bytes 23556 | tf_op jit(solution)/shard_map/while/body/eval_jaxpr/dot_general | solution.py:73
  83.1 2.5 %fusion.54 = f32[2,1280]{1,0:T(2,128)S(1)} fusion(s32[1024]{0:T(1024)S(1)} %dynamic_slice.94, pred[1024]{0:T(1024)(128)(4,1)S(1)} %dynamic_slice.95, f32[2,8192]{1,0:T(2,128)S(1)} %get-tuple-element.615, s32[]{:T(128)S(6)} %select_n.142), kind=kOutput, calls=%fused_computation.13.clone.1 | convolution fusion | flops 34078720 | bytes 23556 | tf_op jit(solution)/shard_map/while/body/eval_jaxpr/dot_general | solution.py:73
  91.2 6.2 %all-gather.9 = f32[4,1,1280]{2,1,0:T(1,128)S(1)} all-gather(f32[1,1,1280]{2,1,0:T(1,128)S(1)} %reshape.51), channel_id=6, replica_groups=mesh['dom'=8,'rep'=4] {'rep'}, dimensions={0}, use_global_device_ids=true | all-gather | bytes 25600 | tf_op jit(solution)/shard_map/all_gather | solution.py:18
  97.5 5.4 %all-gather.8 = f32[4,1,1280]{2,1,0:T(1,128)S(1)} all-gather(f32[1,1,1280]{2,1,0:T(1,128)S(1)} %reshape.49), channel_id=5, replica_groups=mesh['dom'=8,'rep'=4] {'rep'}, dimensions={0}, use_global_device_ids=true | all-gather | bytes 25600 | tf_op jit(solution)/shard_map/all_gather | solution.py:18
  103.0 5.2 %all-gather.7 = s32[4,1,1280]{2,1,0:T(1,128)S(1)} all-gather(s32[1,1,1280]{2,1,0:T(1,128)S(1)} %reshape.47), channel_id=4, replica_groups=mesh['dom'=8,'rep'=4] {'rep'}, dimensions={0}, use_global_device_ids=true | all-gather | bytes 25600 | tf_op jit(solution)/shard_map/all_gather | solution.py:18
  108.2 5.2 %all-gather.6 = s32[4,1,1280]{2,1,0:T(1,128)S(1)} all-gather(s32[1,1,1280]{2,1,0:T(1,128)S(1)} %reshape.45), channel_id=3, replica_groups=mesh['dom'=8,'rep'=4] {'rep'}, dimensions={0}, use_global_device_ids=true | all-gather | bytes 25600 | tf_op jit(solution)/shard_map/all_gather | solution.py:18
  113.5 5.2 %all-gather.5 = f32[4,1,1280]{2,1,0:T(1,128)S(1)} all-gather(f32[1,1,1280]{2,1,0:T(1,128)S(1)} %reshape.43), channel_id=2, replica_groups=mesh['dom'=8,'rep'=4] {'rep'}, dimensions={0}, use_global_device_ids=true | all-gather | bytes 25600 | tf_op jit(solution)/shard_map/all_gather | solution.py:18
  119.4 1.8 %collective-permute-start.4 = (f32[256]{0:T(256)S(1)}, f32[256]{0:T(256)S(1)}, u32[]{:S(2)}, u32[]{:S(2)}) collective-permute-start(f32[256]{0:T(256)S(1)} %slice.112), channel_id=1, source_target_pairs={{0,4},{4,8},{8,12},{12,16},{16,20},{20,24},{24,28},{28,0},{1,5},{5... | collective-permute-start | bytes 3080 | tf_op jit(solution)/shard_map/ppermute | solution.py:27
  121.1 1.5 collective-permute-start.3
  124.2 1.5 collective-permute-start
  125.7 1.5 collective-permute-start.1
  127.2 6.3 %fusion.22 = bf16[64,8192]{1,0:T(8,128)(2,1)} fusion(bf16[64,256]{1,0:T(8,128)(2,1)S(1)} %copy-done.4, f32[256,8192]{1,0:T(8,128)} %copy-done.1, f32[8192]{0:T(1024)S(1)} %copy-done.5, f32[256]{0:T(256)S(1)} %copy-done.6, pred[8192]{0:T(1024)(128)(4,1)S(1)} %get-tuple-element.656), kind=kOutput, calls=%fused_computation.36 | convolution fusion | flops 283639808 | bytes 9511936 | tf_op jit(solution)/shard_map/dot_general | solution.py:114
  139.2 20.8 %all-reduce = (f32[]{:T(128)}, f32[]{:T(128)}) all-reduce(f32[]{:T(128)S(6)} %reduce_sum.46, f32[]{:T(128)S(6)} %reduce_sum.49), channel_id=1, replica_groups=mesh['dom'=8,'rep'=4] {'dom'}, use_global_device_ids=true, to_apply=%region_12.13 | all-reduce | flops 2 | bytes 16 | tf_op jit(solution)/shard_map/psum | solution.py:131
  (191 shorter events, 56.7 us)
Async XLA Ops:
  0.6 7.2 %copy-start = (bf16[64,8192]{1,0:T(8,128)(2,1)S(1)}, bf16[64,8192]{1,0:T(8,128)(2,1)}, u32[]{:S(2)}) copy-start(bf16[64,8192]{1,0:T(8,128)(2,1)} %param.18) | copy-start | bytes 3145732
  0.6 6.6 %copy-start.6 = (f32[256]{0:T(256)S(1)}, f32[256]{0:T(256)}, u32[]{:S(2)}) copy-start(f32[256]{0:T(256)} %param.20) | copy-start | bytes 3076
  0.7 7.2 %copy-start.3 = (bf16[64,256]{1,0:T(8,128)(2,1)S(1)}, bf16[64,256]{1,0:T(8,128)(2,1)}, u32[]{:S(2)}) copy-start(bf16[64,256]{1,0:T(8,128)(2,1)} %param.16) | copy-start | bytes 98308
  0.7 7.1 %copy-start.2 = (f32[8192]{0:T(1024)S(1)}, f32[8192]{0:T(1024)}, u32[]{:S(2)}) copy-start(f32[8192]{0:T(1024)} %param.19) | copy-start | bytes 98308
  12.6 3.2 %copy-start.1 = (f32[256,8192]{1,0:T(8,128)}, f32[256,8192]{1,0:T(8,128)S(1)}, u32[]{:S(2)}) copy-start(f32[256,8192]{1,0:T(8,128)S(1)} %get-tuple-element.406) | copy-start | bytes 25165828
  12.6 7.6 %copy-start.5 = (f32[8192]{0:T(1024)S(1)}, f32[8192]{0:T(1024)}, u32[]{:S(2)}) copy-start(f32[8192]{0:T(1024)} %param.21) | copy-start | bytes 98308
  21.0 106.2 %copy-start.4 = (bf16[64,256]{1,0:T(8,128)(2,1)S(1)}, bf16[64,256]{1,0:T(8,128)(2,1)}, u32[]{:S(2)}) copy-start(bf16[64,256]{1,0:T(8,128)(2,1)} %param.15) | copy-start | bytes 98308
  119.4 15.4 %collective-permute-start.4 = (f32[256]{0:T(256)S(1)}, f32[256]{0:T(256)S(1)}, u32[]{:S(2)}, u32[]{:S(2)}) collective-permute-start(f32[256]{0:T(256)S(1)} %slice.112), channel_id=1, source_target_pairs={{0,4},{4,8},{8,12},{12,16},{16,20},{20,24},{24,28},{28,0},{1,5},{5... | collective-permute-start | bytes 3080 | tf_op jit(solution)/shard_map/ppermute | solution.py:27
  121.1 13.0 %collective-permute-start.3 = (f32[256]{0:T(256)S(1)}, f32[256]{0:T(256)S(1)}, u32[]{:S(2)}, u32[]{:S(2)}) collective-permute-start(f32[256]{0:T(256)S(1)} %slice.109), channel_id=1, source_target_pairs={{0,4},{4,8},{8,12},{12,16},{16,20},{20,24},{24,28},{28,0},{1,5},{5... | collective-permute-start | bytes 3080 | tf_op jit(solution)/shard_map/ppermute | solution.py:27
  122.7 38.7 %collective-permute-start.2 = (f32[256]{0:T(256)S(1)}, f32[256]{0:T(256)S(1)}, u32[]{:S(2)}, u32[]{:S(2)}) collective-permute-start(f32[256]{0:T(256)S(1)} %slice.105), channel_id=1, source_target_pairs={{0,4},{4,8},{8,12},{12,16},{16,20},{20,24},{24,28},{28,0},{1,5},{5... | collective-permute-start | bytes 3080 | tf_op jit(solution)/shard_map/ppermute | solution.py:27
  124.2 13.7 %collective-permute-start = (s32[256]{0:T(256)S(1)}, s32[256]{0:T(256)S(1)}, u32[]{:S(2)}, u32[]{:S(2)}) collective-permute-start(s32[256]{0:T(256)S(1)} %slice.99), channel_id=1, source_target_pairs={{0,4},{4,8},{8,12},{12,16},{16,20},{20,24},{24,28},{28,0},{1,5},{5... | collective-permute-start | bytes 3080 | tf_op jit(solution)/shard_map/ppermute | solution.py:27
  125.7 12.2 %collective-permute-start.1 = (s32[256]{0:T(256)S(1)}, s32[256]{0:T(256)S(1)}, u32[]{:S(2)}, u32[]{:S(2)}) collective-permute-start(s32[256]{0:T(256)S(1)} %slice.101), channel_id=1, source_target_pairs={{0,4},{4,8},{8,12},{12,16},{16,20},{20,24},{24,28},{28,0},{1,5},{5... | collective-permute-start | bytes 3080 | tf_op jit(solution)/shard_map/ppermute | solution.py:27
where the time goes:
time: 164 us; the launch traced here: 163 us
  blocking collectives  48.1 us (29%)
  other arithmetic  42.5 us (26%)
  matrix products  41.6 us (25%)
  local copies, waits for them, and re-layouts  15.3 us (9%)
  starting transfers between devices  7.87 us (5%)
  between operations  6.72 us (4%)
    all_gather x5, blocking collectives, combined_all(): pieces = jax.tree.map(lambda part: lax.all_gather(part, axis), value)  27.3 us
    psum x1, blocking collectives, shards(): gap_total, area_total = lax.psum((jnp.sum(own[3]), jnp.sum(own[4])), 'dom')  20.8 us
    dot_general x8, matrix products, one_block(): lax.dot_general(take(paired), hit.astype(jnp.float32), (((1,), (1,)), (()...  20.4 us
    dynamic_slice x32, local copies, waits for them, and re-layouts, take(): return lax.dynamic_slice_in_dim(values, begin, block_len, values.ndim - 1)  11.2 us
    dot_general x2, matrix products, project(): lax.dot_general(shape_table, displace, (((0,), (0,)), ((), ())), preferre...  10.5 us
    reduce_max x8, other arithmetic, one_block(): best_rank = jnp.max(jnp.where(hit, block_ranks[None, :], -1), axis=1)  10.2 us
    reduce_max x8, other arithmetic, one_block(): jnp.max(jnp.where(hit, take(row_pen)[None, :], LOWEST_FILL), axis=1)  8.89 us
    ppermute x5, starting transfers between devices, passed_along(): lax.ppermute(x, axis, [(i, (i + by) % length) for i in range(length)])  7.87 us
  transfers between devices with their start and end apart: 5, of which 0 were waited for; matrix products, arithmetic and copies ran while one was open for 6% of the time, Pallas kernels for 0%

commit v1 on v0

v1 whole, which is shorter than its diff:
```python
import functools

import jax
import jax.numpy as jnp
from jax import lax
from jax.experimental import pallas as pl
from jax.experimental.pallas import tpu as pltpu
from jax.sharding import PartitionSpec as P

SEG_DEV = 1024
SPILL = 256


PENALTY = 400.0
LOWEST_FILL = -1e30
FACE_LIMIT = 1073741824
LANES = 128
GROUP = 16
NO_KEY = -(2**31)


def pieces_of(value, count):
    parts = []
    for _ in range(count):
        part = value.astype(jnp.bfloat16).astype(jnp.float32)
        parts.append(part)
        value = value - part
    return parts


def local_kernel(
    live_ref,
    ns_ref,
    nm_ref,
    weight_ref,
    sec_ref,
    mst_ref,
    offset_ref,
    jac_ref,
    slot_ref,
    face_ref,
    rank_ref,
    force_ref,
    table_ref,
    table_w,
    wide_weight,
):
    step = pl.program_id(0)
    points = ns_ref.shape[1]
    nodes = ns_ref.shape[0]
    rows = sec_ref.shape[1]
    blocks = rows // LANES
    bf16, f32, i32 = jnp.bfloat16, jnp.float32, jnp.int32

    @pl.when(step == 0)
    def _():
        weight = weight_ref[...]
        ns32, nm32 = ns_ref[...].astype(f32), nm_ref[...].astype(f32)
        wide_weight[...] = jnp.transpose(jnp.broadcast_to(weight, (LANES, points)))
        both = jnp.concatenate([ns32, -nm32], axis=0)
        tops = jnp.sum(both * weight, axis=1, keepdims=True)
        ones_at = lax.broadcasted_iota(i32, (GROUP, points), 0) < 3
        total = jnp.sum(weight, axis=1, keepdims=True)
        tails = jnp.broadcast_to(total, (GROUP, LANES))
        tail_parts = pieces_of(tails, 3)
        top_parts = pieces_of(jnp.broadcast_to(tops, (2 * nodes, LANES)), 3)
        lane = lax.broadcasted_iota(i32, (2 * nodes, LANES), 1)
        head = jnp.where(lane == 0, top_parts[0], jnp.where(lane == 1, top_parts[1], jnp.where(lane == 2, top_parts[2], 0.0)))
        lane = lax.broadcasted_iota(i32, (GROUP, LANES), 1)
        sub = lax.broadcasted_iota(i32, (GROUP, LANES), 0)
        foot = jnp.where(lane == 0, tail_parts[0], jnp.where(lane == 1, tail_parts[1], jnp.where(lane == 2, tail_parts[2], 0.0)))
        foot = jnp.where(sub < 3, foot, 0.0)
        left = jnp.concatenate([both, ones_at.astype(f32)], axis=0)
        right = jnp.concatenate([head, foot], axis=0)
        table_w[0:points, :] = jnp.transpose(left).astype(bf16)
        table_w[points:, :] = jnp.transpose(right).astype(bf16)[0:GROUP, :]
        table_ref[0:GROUP, :] = jnp.full((GROUP, LANES), LOWEST_FILL, f32)
        table_ref[GROUP:, :] = jnp.zeros((table_ref.shape[0] - GROUP, LANES), f32)

    live_count = live_ref[0]
    row_ids = (
        step * rows
        + LANES * lax.broadcasted_iota(i32, (blocks, LANES), 0)
        + lax.broadcasted_iota(i32, (blocks, LANES), 1)
    )
    live = row_ids < live_count
    jac = jac_ref[...]

    def as_row(value):
        return jnp.concatenate([value[b : b + 1, :] for b in range(blocks)], axis=1)

    def as_block(value):
        return jnp.concatenate([value[:, LANES * b : LANES * (b + 1)] for b in range(blocks)], axis=0)

    off = pieces_of(offset_ref[...], 3)
    sub = lax.broadcasted_iota(i32, (GROUP, rows), 0)
    off_rows = jnp.where(
        sub == 0, as_row(off[0]), jnp.where(sub == 1, as_row(off[1]), jnp.where(sub == 2, as_row(off[2]), 0.0))
    ).astype(bf16)
    stacked = jnp.concatenate([sec_ref[...], mst_ref[...], off_rows], axis=0)
    gaps = jnp.dot(table_w[...], stacked, preferred_element_type=f32)
    field = gaps[0:points, :]
    pen = as_block(-jnp.min(field, axis=0, keepdims=True))
    weighted = as_block(gaps[points : points + 1, :] + gaps[points + 1 : points + 2, :] + gaps[points + 2 : points + 3, :])

    weights = wide_weight[...]
    scale = jnp.where(live, jac * -PENALTY, 0.0)
    loads = jnp.concatenate(
        [
            (jnp.minimum(field[:, LANES * b : LANES * (b + 1)], 0.0) * weights).astype(bf16)
            for b in range(blocks)
        ],
        axis=1,
    )
    force = jnp.dot(ns_ref[...], loads, preferred_element_type=f32)
    force_ref[...] = (force * as_row(scale)).astype(bf16)

    row_gap = jnp.where(live, jac * weighted, 0.0)
    row_area = jnp.where(live, jac * jnp.sum(weight_ref[...], axis=1, keepdims=True), 0.0)
    table_ref[5 * GROUP : 5 * GROUP + blocks, :] += row_gap
    table_ref[5 * GROUP + 8 : 5 * GROUP + 8 + blocks, :] += row_area

    slot = jnp.where(live, slot_ref[...], (GROUP - 1) * LANES)
    key = ((rank_ref[...] - 2) << 30) + (FACE_LIMIT - 1 - face_ref[...])
    gap_parts = pieces_of(row_gap, 3)
    slot_t, pen_t, key_t = jnp.transpose(slot), jnp.transpose(pen), jnp.transpose(key)
    sub = lax.broadcasted_iota(i32, (LANES, LANES), 0)
    lane = lax.broadcasted_iota(i32, (LANES, LANES), 1)
    group_id = lax.broadcasted_iota(i32, (GROUP, LANES), 0)
    for b in range(blocks):
        slot_col = jnp.broadcast_to(slot_t[:, b : b + 1], (LANES, LANES))
        slot_row = slot[b : b + 1, :]
        same = slot_col == slot_row
        top_pen = jnp.max(jnp.where(same, pen_t[:, b : b + 1], LOWEST_FILL), axis=0, keepdims=True)
        top_key = jnp.max(jnp.where(same, key_t[:, b : b + 1], NO_KEY), axis=0, keepdims=True)
        last = jnp.max(jnp.where(same, sub, -1), axis=0, keepdims=True)
        speaks = last == lax.broadcasted_iota(i32, (1, LANES), 1)
        home = (slot_row >> 7) == group_id
        spoken = home & speaks
        one_hot = jnp.where((slot_col & (LANES - 1)) == lane, 1.0, 0.0).astype(bf16)
        values = pieces_of(top_pen, 3) + [
            (top_key & 255).astype(f32),
            ((top_key >> 8) & 255).astype(f32),
            ((top_key >> 16) & 255).astype(f32),
            (top_key >> 24).astype(f32),
        ]
        picks = [jnp.where(spoken, value, 0.0) for value in values]
        picks.append(jnp.where(spoken, 1.0, 0.0))
        picks += [jnp.where(home, part[b : b + 1, :], 0.0) for part in gap_parts]
        left = jnp.concatenate(picks, axis=0).astype(bf16)
        out = jnp.dot(left, one_hot, preferred_element_type=f32)
        part = [out[GROUP * i : GROUP * (i + 1), :] for i in range(11)]
        there = part[7] > 0.5
        fresh_pen = jnp.where(there, (part[0] + part[1]) + part[2], LOWEST_FILL)
        fresh_high = part[6] * 256.0 + part[5]
        fresh_low = part[4] * 256.0 + part[3]
        old_pen = table_ref[0:GROUP, :]
        old_high = table_ref[GROUP : 2 * GROUP, :]
        old_low = table_ref[2 * GROUP : 3 * GROUP, :]
        fresh_wins = there & (
            (old_pen == LOWEST_FILL)
            | (fresh_high > old_high)
            | ((fresh_high == old_high) & (fresh_low > old_low))
        )
        table_ref[0:GROUP, :] = jnp.maximum(old_pen, fresh_pen)
        table_ref[GROUP : 2 * GROUP, :] = jnp.where(fresh_wins, fresh_high, old_high)
        table_ref[2 * GROUP : 3 * GROUP, :] = jnp.where(fresh_wins, fresh_low, old_low)
        table_ref[3 * GROUP : 4 * GROUP, :] += (part[8] + part[9]) + part[10]


def local_step(ns, nm, sec, mst, offset, weight, jac, slot, face, rank, live):
    nodes, points = ns.shape
    row_count = sec.shape[1]
    rows = min(row_count, 1024)
    folded = lambda value: value.reshape(row_count // LANES, LANES)
    whole = lambda shape: pl.BlockSpec(shape, lambda i: (0, 0))
    wide = pl.BlockSpec((nodes, rows), lambda i: (0, i))
    tall = pl.BlockSpec((rows // LANES, LANES), lambda i: (i, 0))
    return pl.pallas_call(
        local_kernel,
        grid=(row_count // rows,),
        in_specs=[
            pl.BlockSpec(memory_space=pltpu.SMEM),
            whole((nodes, points)),
            whole((nodes, points)),
            whole((1, points)),
            wide,
            wide,
            tall,
            tall,
            tall,
            tall,
            tall,
        ],
        out_specs=[wide, whole((6 * GROUP, LANES))],
        out_shape=[
            jax.ShapeDtypeStruct((nodes, row_count), jnp.bfloat16),
            jax.ShapeDtypeStruct((6 * GROUP, LANES), jnp.float32),
        ],
        scratch_shapes=[
            pltpu.VMEM((points + GROUP, 2 * nodes + GROUP), jnp.bfloat16),
            pltpu.VMEM((points, LANES), jnp.float32),
        ],
    )(
        live,
        ns,
        nm,
        weight.reshape(1, points),
        sec,
        mst,
        folded(offset),
        folded(jac),
        folded(slot),
        folded(face),
        folded(rank),
    )


def sent(value, dom_by, rep_by):
    doms, reps = lax.axis_size("dom"), lax.axis_size("rep")
    pairs = [
        (d * reps + r, (d + dom_by) % doms * reps + (r + rep_by) % reps)
        for d in range(doms)
        for r in range(reps)
    ]
    return lax.ppermute(value, ("dom", "rep"), pairs)


def merge(first, second):
    wins = (second[1] > first[1]) | ((second[1] == first[1]) & (second[2] > first[2]))
    wins = (second[0] > LOWEST_FILL) & (wins | (first[0] <= LOWEST_FILL))
    return (
        jnp.maximum(first[0], second[0]),
        jnp.where(wins, second[1], first[1]),
        jnp.where(wins, second[2], first[2]),
        first[3] + second[3],
    )


def shards(ns, nm, sec, mst, offset, weight, jac, slot, face, rank, live):
    doms, reps = lax.axis_size("dom"), lax.axis_size("rep")
    own_rows, spill_rows = SEG_DEV // LANES, SPILL // LANES
    force, table = local_step(ns, nm, sec, mst, offset, weight, jac, slot, face, rank, live)
    planes = [table[GROUP * i : GROUP * (i + 1)] for i in range(4)]
    totals = jnp.stack([jnp.sum(table[5 * GROUP : 5 * GROUP + 8]), jnp.sum(table[5 * GROUP + 8 :])])
    totals = jnp.pad(totals, (0, LANES - 2)).reshape(1, LANES)
    own = jnp.concatenate([plane[:own_rows] for plane in planes] + [totals], axis=0)
    spill = jnp.concatenate([plane[own_rows : own_rows + spill_rows] for plane in planes], axis=0)

    mates = [own] + [sent(own, 0, k) for k in range(1, reps)]
    arrivals = [sent(spill, 1, k) for k in range(reps)]
    split = lambda value, rows: tuple(value[rows * i : rows * (i + 1)] for i in range(4))
    merged = functools.reduce(merge, [split(value, own_rows) for value in mates])
    lead = functools.reduce(merge, [split(value, spill_rows) for value in arrivals])
    lead = merge(tuple(part[:spill_rows] for part in merged), lead)
    pen, high, low, gap = (
        jnp.concatenate([head, part[spill_rows:]], axis=0) for head, part in zip(lead, merged)
    )
    empty = pen <= LOWEST_FILL
    key = high.astype(jnp.int32) * 65536 + low.astype(jnp.int32)
    seg_face = jnp.where(empty, -1, FACE_LIMIT - 1 - (key & (FACE_LIMIT - 1)))
    seg_pen = jnp.where(empty, 0.0, pen)

    group = functools.reduce(jnp.add, [value[4 * own_rows :] for value in mates])
    reach = 1
    while reach < doms:
        group = group + sent(group, reach, 0)
        reach *= 2
    mean_gap = group[0, 0] / group[0, 1]
    return (force, seg_pen.reshape(-1), seg_face.reshape(-1), gap.reshape(-1), mean_gap)


def solution(mesh):
    return jax.shard_map(
        shards,
        mesh=mesh,
        in_specs=(
            P(),
            P(),
            P(None, ("dom", "rep")),
            P(None, ("dom", "rep")),
            P(("dom", "rep")),
            P(),
            P(("dom", "rep")),
            P(("dom", "rep")),
            P(("dom", "rep")),
            P(("dom", "rep")),
            P(("dom", "rep")),
        ),
        out_specs=(P(None, ("dom", "rep")), P("dom"), P("dom"), P("dom"), P()),
        check_vma=False,
    )
```

time: 164 us -> 50.3 us (0.31)
  blocking collectives: 48.1 us -> 0 us
  matrix products: 41.6 us -> 0 us
  other arithmetic: 42.5 us -> 5.26 us
  waiting for transfers between devices: 0.01 us -> 13.3 us
  local copies, waits for them, and re-layouts: 15.3 us -> 3.42 us
  Pallas kernels: 0 us -> 11.4 us
  starting transfers between devices: 7.87 us -> 12.7 us
  between operations: 6.72 us -> 3.83 us
    dot_general x12 -> x0, matrix products: 41.6 us -> none  [the longest x8 20.4 us: one_block(): lax.dot_general(take(paired), hit.astype(jnp.float32), (((1,), (1,)), (()...]
    all_gather x5 -> x0, blocking collectives: 27.3 us -> none  [combined_all(): pieces = jax.tree.map(lambda part: lax.all_gather(part, axis), value)]
    reduce_max x24 -> x0, other arithmetic: 25.4 us -> none  [the longest x8 10.2 us: one_block(): best_rank = jnp.max(jnp.where(hit, block_ranks[None, :], -1), axis=1)]
    psum x1 -> x0, blocking collectives: 20.8 us -> none  [shards(): gap_total, area_total = lax.psum((jnp.sum(own[3]), jnp.sum(own[4])), 'dom')]
    ppermute x5 -> x10, waiting for transfers between devices: 0.01 us -> 13.3 us  [sent(): return lax.ppermute(value, ('dom', 'rep'), pairs)]
    dynamic_slice x41 -> x0, local copies, waits for them, and re-layouts: 11.5 us -> none  [the longest x32 11.2 us: take(): return lax.dynamic_slice_in_dim(values, begin, block_len, values.ndim - 1)]
    pallas_call x0 -> x1, Pallas kernels: none -> 11.4 us  [local_step(): pl.pallas_call(local_kernel, grid=(row_count // rows,), in_specs=[pl.Bloc...]
    reduce_min x8 -> x0, other arithmetic: 6.13 us -> none  [one_block(): jnp.min(jnp.where(member, chosen[None, :], FACE_LIMIT), axis=1)]
  transfers between devices with their start and end apart: 5 -> 10, of which waited for: 0 -> 4; matrix products, arithmetic and copies ran while one was open for 6% -> 15% of each run, Pallas kernels for 0% -> 0%
where the time goes in v1:
time: 50.3 us; the launch traced here: 49.9 us
  waiting for transfers between devices  13.3 us (26%)
  starting transfers between devices  12.7 us (25%)
  Pallas kernels  11.4 us (23%)
  other arithmetic  5.26 us (10%)
  between operations  3.83 us (8%)
  local copies, waits for them, and re-layouts  3.42 us (7%)
    ppermute x10, waiting for transfers between devices, sent(): return lax.ppermute(value, ('dom', 'rep'), pairs)  13.3 us
    ppermute x10, starting transfers between devices, sent(): return lax.ppermute(value, ('dom', 'rep'), pairs)  12.7 us
    pallas_call x1, Pallas kernels, local_step(): pl.pallas_call(local_kernel, grid=(row_count // rows,), in_specs=[pl.Bloc...  11.4 us
    unnamed x5, local copies, waits for them, and re-layouts  2.05 us
    add x1, other arithmetic, shards(): group = functools.reduce(jnp.add, [value[4 * own_rows:] for value in mates])  1.37 us
    reshape x1, other arithmetic, shards(): totals = jnp.pad(totals, (0, LANES - 2)).reshape(1, LANES)  1.37 us
  transfers between devices with their start and end apart: 10, of which 4 were waited for; matrix products, arithmetic and copies ran while one was open for 15% of the time, Pallas kernels for 0%

profile of v1, /device:TPU:0, one launch (start us, length us, event | category | flops | bytes accessed | tf_op | source)
XLA Modules:
  0.0 49.9 jit_solution(13616827031802647872)
XLA Ops:
  1.3 11.4 %shard_map.146 = (bf16[64,8192]{1,0:T(8,128)(2,1)}, f32[96,128]{1,0:T(8,128)}) custom-call(s32[1]{0:T(128)S(6)} %copy.20.live_ref, bf16[64,256]{1,0:T(8,128)(2,1)} %ns_ref.1, bf16[64,256]{1,0:T(8,128)(2,1)} %nm_ref.1, f32[1,256]{1,0:T(1,128)} %bitcast.30, bf16[64,8192]{1,0:T(8,128)(2,1)} %sec_ref.1, bf16[64,8192]{1,0:T(8,128)(2,1)} %mst_ref.1, ...), custom_call_target="tpu_custom_call" | custom-call | tf_op jit(solution)/shard_map/pallas_call | solution.py:179
  12.7 0.8 %fusion.7 = (f32[2,128]{1,0:T(2,128)S(1)}, f32[2,128]{1,0:T(2,128)S(1)}, f32[2,128]{1,0:T(2,128)S(1)}, f32[2,128]{1,0:T(2,128)S(1)}) fusion(f32[96,128]{1,0:T(8,128)} %get-tuple-element.8), kind=kLoop, calls=%fused_computation.57 | loop fusion | bytes 8192 | tf_op jit(solution)/shard_map/slice | solution.py:248
  13.5 4.0 %collective-permute-start.5 = (f32[8,128]{1,0:T(8,128)S(1)}, f32[8,128]{1,0:T(8,128)S(1)}, u32[]{:S(2)}, u32[]{:S(2)}) collective-permute-start(f32[8,128]{1,0:T(8,128)S(1)} %pad_maximum_fusion), channel_id=1, source_target_pairs={{0,6},{1,7},{2,4},{3,5},{4,10},{5,11},{6,8},{7,9},{8,14},{9,15},{1... | collective-permute-start | bytes 12296 | tf_op jit(solution)/shard_map/ppermute | solution.py:226
  17.5 1.5 %collective-permute-start.3 = (f32[8,128]{1,0:T(8,128)S(1)}, f32[8,128]{1,0:T(8,128)S(1)}, u32[]{:S(2)}, u32[]{:S(2)}) collective-permute-start(f32[8,128]{1,0:T(8,128)S(1)} %pad_maximum_fusion), channel_id=1, source_target_pairs={{0,4},{1,5},{2,6},{3,7},{4,8},{5,9},{6,10},{7,11},{8,12},{9,13},{1... | collective-permute-start | bytes 12296 | tf_op jit(solution)/shard_map/ppermute | solution.py:226
  19.0 0.4 collective-permute-start.4
  19.4 0.7 %constant_dynamic-update-slice_fusion.3 = f32[33,128]{1,0:T(8,128)S(1)} fusion(f32[96,128]{1,0:T(8,128)} %get-tuple-element.8), kind=kLoop, calls=%fused_computation.3 | loop fusion | bytes 8192
  20.1 0.7 %constant_dynamic-update-slice_fusion.2 = f32[33,128]{1,0:T(8,128)S(1)} fusion(f32[33,128]{1,0:T(8,128)S(1)} %constant_dynamic-update-slice_fusion.3, f32[96,128]{1,0:T(8,128)} %get-tuple-element.8), kind=kLoop, calls=%fused_computation.2 | loop fusion | bytes 8192
  20.7 0.7 %constant_dynamic-update-slice_fusion.1 = f32[33,128]{1,0:T(8,128)S(1)} fusion(f32[33,128]{1,0:T(8,128)S(1)} %constant_dynamic-update-slice_fusion.2, f32[96,128]{1,0:T(8,128)} %get-tuple-element.8), kind=kLoop, calls=%fused_computation.1 | loop fusion | bytes 8192
  21.4 0.6 %slice_reduce_fusion.1 = (f32[]{:T(128)}, f32[]{:T(128)}, f32[33,128]{1,0:T(8,128)S(1)}) fusion(f32[96,128]{1,0:T(8,128)S(1)} %copy-done, f32[33,128]{1,0:T(8,128)S(1)} %constant_dynamic-update-slice_fusion.1), kind=kLoop, calls=%fused_computation.20 | loop fusion | flops 2046 | bytes 16392 | tf_op jit(solution)/shard_map/reduce_sum | solution.py:245
  22.0 1.4 %fusion.6 = f32[1,128]{1,0:T(1,128)S(1)} fusion(f32[1]{0:T(128)} %bitcast.7, f32[1]{0:T(128)} %bitcast.6), kind=kLoop, calls=%fused_computation.56 | loop fusion | flops 512 | bytes 520 | tf_op jit(solution)/shard_map/reshape | solution.py:246
  23.4 0.6 %collective-permute-start.1 = (f32[33,128]{1,0:T(8,128)S(1)}, f32[33,128]{1,0:T(8,128)S(1)}, u32[]{:S(2)}, u32[]{:S(2)}) collective-permute-start(f32[33,128]{1,0:T(8,128)S(1)} %dynamic-update-slice.4), channel_id=1, source_target_pairs={{0,2},{1,3},{2,0},{3,1},{4,6},{5,7},{6,4},{7,5},{8,10},{9,11},{10,... | collective-permute-start | bytes 50696 | tf_op jit(solution)/shard_map/ppermute | solution.py:226
  24.0 2.0 %collective-permute-start.2 = (f32[33,128]{1,0:T(8,128)S(1)}, f32[33,128]{1,0:T(8,128)S(1)}, u32[]{:S(2)}, u32[]{:S(2)}) collective-permute-start(f32[33,128]{1,0:T(8,128)S(1)} %dynamic-update-slice.4), channel_id=1, source_target_pairs={{0,3},{1,0},{2,1},{3,2},{4,7},{5,4},{6,5},{7,6},{8,11},{9,8},{10,9... | collective-permute-start | bytes 50696 | tf_op jit(solution)/shard_map/ppermute | solution.py:226
  26.0 0.0 collective-permute-done.3
  26.0 2.7 %collective-permute-start.6 = (f32[8,128]{1,0:T(8,128)S(1)}, f32[8,128]{1,0:T(8,128)S(1)}, u32[]{:S(2)}, u32[]{:S(2)}) collective-permute-start(f32[8,128]{1,0:T(8,128)S(1)} %pad_maximum_fusion), channel_id=1, source_target_pairs={{0,7},{1,4},{2,5},{3,6},{4,11},{5,8},{6,9},{7,10},{8,15},{9,12},{1... | collective-permute-start | bytes 12296 | tf_op jit(solution)/shard_map/ppermute | solution.py:226
  28.8 0.6 %collective-permute-done = f32[33,128]{1,0:T(8,128)S(1)} collective-permute-done((f32[33,128]{1,0:T(8,128)S(1)}, f32[33,128]{1,0:T(8,128)S(1)}, u32[]{:S(2)}, u32[]{:S(2)}) %collective-permute-start) | collective-permute-done | bytes 16928 | tf_op jit(solution)/shard_map/ppermute | solution.py:226
  29.4 1.4 %slice_add_fusion.3 = f32[1,128]{1,0:T(1,128)S(1)} fusion(f32[33,128]{1,0:T(8,128)S(1)} %collective-permute-done.2, f32[33,128]{1,0:T(8,128)S(1)} %collective-permute-done.1, f32[33,128]{1,0:T(8,128)S(1)} %collective-permute-done, f32[1]{0:T(128)} %bitcast.7, f32[1]{0:T(128)} %bitcast.6), kind=kLoop, calls=%fused_computation.53 | loop fusion | flops 896 | bytes 2056 | tf_op jit(solution)/shard_map/add | solution.py:264
  30.8 1.5 %collective-permute-start.7 = (f32[1,128]{1,0:T(1,128)S(1)}, f32[1,128]{1,0:T(1,128)S(1)}, u32[]{:S(2)}, u32[]{:S(2)}) collective-permute-start(f32[1,128]{1,0:T(1,128)S(1)} %slice_add_fusion.3), channel_id=1, source_target_pairs={{0,4},{1,5},{2,6},{3,7},{4,8},{5,9},{6,10},{7,11},{8,12},{9,13},{1... | collective-permute-start | bytes 1544 | tf_op jit(solution)/shard_map/ppermute | solution.py:226
  32.4 0.6 %maximum_bitcast_fusion.1 = f32[1024]{0:T(1024)} fusion(f32[6,128]{1,0:T(8,128)S(1)} %slice.210, f32[2,128]{1,0:T(2,128)S(1)} %get-tuple-element.33), kind=kLoop, calls=%fused_computation.18 | loop fusion | flops 1024 | bytes 8192 | tf_op jit(solution)/shard_map/reshape | solution.py:270
  33.1 4.0 %collective-permute-done.7 = f32[1,128]{1,0:T(1,128)S(1)} collective-permute-done((f32[1,128]{1,0:T(1,128)S(1)}, f32[1,128]{1,0:T(1,128)S(1)}, u32[]{:S(2)}, u32[]{:S(2)}) %collective-permute-start.7) | collective-permute-done | bytes 544 | tf_op jit(solution)/shard_map/ppermute | solution.py:226
  37.1 0.6 %compare_select_fusion.1 = f32[1024]{0:T(1024)} fusion(f32[6,128]{1,0:T(8,128)S(1)} %slice.183, f32[2,128]{1,0:T(2,128)S(1)} %get-tuple-element.34), kind=kLoop, calls=%fused_computation.5 | loop fusion | flops 3072 | bytes 8192 | tf_op jit(solution)/shard_map/jit(_where)/select_n | solution.py:262
  37.7 4.8 %collective-permute-done.8 = f32[1,128]{1,0:T(1,128)S(1)} collective-permute-done((f32[1,128]{1,0:T(1,128)S(1)}, f32[1,128]{1,0:T(1,128)S(1)}, u32[]{:S(2)}, u32[]{:S(2)}) %collective-permute-start.8) | collective-permute-done | bytes 544 | tf_op jit(solution)/shard_map/ppermute | solution.py:226
  42.4 0.6 %compare_select_fusion = s32[1024]{0:T(1024)} fusion(f32[6,128]{1,0:T(8,128)S(1)} %slice.200, f32[2,128]{1,0:T(2,128)S(1)} %slice_select_fusion.7, f32[6,128]{1,0:T(8,128)S(1)} %slice.201, f32[2,128]{1,0:T(2,128)S(1)} %get-tuple-element.11, f32[6,128]{1,0:T(8,128)S(1)} %slice.183, f32[2,128]{1,0:T(2,128)S(1)} %get-tuple-element.34), kind=kLoop, calls=%fused_computation.4 | loop fusion | flops 11264 | bytes 16384 | tf_op jit(solution)/shard_map/jit(_where)/select_n | solution.py:261
  43.0 3.9 %collective-permute-done.9 = f32[1,128]{1,0:T(1,128)S(1)} collective-permute-done((f32[1,128]{1,0:T(1,128)S(1)}, f32[1,128]{1,0:T(1,128)S(1)}, u32[]{:S(2)}, u32[]{:S(2)}) %collective-permute-start.9) | collective-permute-done | bytes 544 | tf_op jit(solution)/shard_map/ppermute | solution.py:226
  46.9 0.6 %fusion.8 = (f32[1,1]{1,0:T(1,128)}, f32[1,1]{1,0:T(1,128)}) fusion(f32[1,128]{1,0:T(1,128)S(1)} %add.59), kind=kLoop, calls=%fused_computation.58 | loop fusion | bytes 16 | tf_op jit(solution)/shard_map/slice | solution.py:269
  (26 shorter events, 0.2 us)
Async XLA Ops:
  12.7 8.7 %copy-start = (f32[96,128]{1,0:T(8,128)S(1)}, f32[96,128]{1,0:T(8,128)}, u32[]{:S(2)}) copy-start(f32[96,128]{1,0:T(8,128)} %get-tuple-element.8) | copy-start | bytes 147460
  13.5 12.6 %collective-permute-start.5 = (f32[8,128]{1,0:T(8,128)S(1)}, f32[8,128]{1,0:T(8,128)S(1)}, u32[]{:S(2)}, u32[]{:S(2)}) collective-permute-start(f32[8,128]{1,0:T(8,128)S(1)} %pad_maximum_fusion), channel_id=1, source_target_pairs={{0,6},{1,7},{2,4},{3,5},{4,10},{5,11},{6,8},{7,9},{8,14},{9,15},{1... | collective-permute-start | bytes 12296 | tf_op jit(solution)/shard_map/ppermute | solution.py:226
  17.5 8.6 %collective-permute-start.3 = (f32[8,128]{1,0:T(8,128)S(1)}, f32[8,128]{1,0:T(8,128)S(1)}, u32[]{:S(2)}, u32[]{:S(2)}) collective-permute-start(f32[8,128]{1,0:T(8,128)S(1)} %pad_maximum_fusion), channel_id=1, source_target_pairs={{0,4},{1,5},{2,6},{3,7},{4,8},{5,9},{6,10},{7,11},{8,12},{9,13},{1... | collective-permute-start | bytes 12296 | tf_op jit(solution)/shard_map/ppermute | solution.py:226
  19.0 9.8 %collective-permute-start.4 = (f32[8,128]{1,0:T(8,128)S(1)}, f32[8,128]{1,0:T(8,128)S(1)}, u32[]{:S(2)}, u32[]{:S(2)}) collective-permute-start(f32[8,128]{1,0:T(8,128)S(1)} %pad_maximum_fusion), channel_id=1, source_target_pairs={{0,5},{1,6},{2,7},{3,4},{4,9},{5,10},{6,11},{7,8},{8,13},{9,14},{1... | collective-permute-start | bytes 12296 | tf_op jit(solution)/shard_map/ppermute | solution.py:226
  23.4 5.3 %collective-permute-start.1 = (f32[33,128]{1,0:T(8,128)S(1)}, f32[33,128]{1,0:T(8,128)S(1)}, u32[]{:S(2)}, u32[]{:S(2)}) collective-permute-start(f32[33,128]{1,0:T(8,128)S(1)} %dynamic-update-slice.4), channel_id=1, source_target_pairs={{0,2},{1,3},{2,0},{3,1},{4,6},{5,7},{6,4},{7,5},{8,10},{9,11},{10,... | collective-permute-start | bytes 50696 | tf_op jit(solution)/shard_map/ppermute | solution.py:226
  24.0 4.8 %collective-permute-start.2 = (f32[33,128]{1,0:T(8,128)S(1)}, f32[33,128]{1,0:T(8,128)S(1)}, u32[]{:S(2)}, u32[]{:S(2)}) collective-permute-start(f32[33,128]{1,0:T(8,128)S(1)} %dynamic-update-slice.4), channel_id=1, source_target_pairs={{0,3},{1,0},{2,1},{3,2},{4,7},{5,4},{6,5},{7,6},{8,11},{9,8},{10,9... | collective-permute-start | bytes 50696 | tf_op jit(solution)/shard_map/ppermute | solution.py:226
  26.0 3.4 %collective-permute-start = (f32[33,128]{1,0:T(8,128)S(1)}, f32[33,128]{1,0:T(8,128)S(1)}, u32[]{:S(2)}, u32[]{:S(2)}) collective-permute-start(f32[33,128]{1,0:T(8,128)S(1)} %dynamic-update-slice.4), channel_id=1, source_target_pairs={{0,1},{1,2},{2,3},{3,0},{4,5},{5,6},{6,7},{7,4},{8,9},{9,10},{10,1... | collective-permute-start | bytes 50696 | tf_op jit(solution)/shard_map/ppermute | solution.py:226
  26.0 6.3 %collective-permute-start.6 = (f32[8,128]{1,0:T(8,128)S(1)}, f32[8,128]{1,0:T(8,128)S(1)}, u32[]{:S(2)}, u32[]{:S(2)}) collective-permute-start(f32[8,128]{1,0:T(8,128)S(1)} %pad_maximum_fusion), channel_id=1, source_target_pairs={{0,7},{1,4},{2,5},{3,6},{4,11},{5,8},{6,9},{7,10},{8,15},{9,12},{1... | collective-permute-start | bytes 12296 | tf_op jit(solution)/shard_map/ppermute | solution.py:226
  30.8 6.3 %collective-permute-start.7 = (f32[1,128]{1,0:T(1,128)S(1)}, f32[1,128]{1,0:T(1,128)S(1)}, u32[]{:S(2)}, u32[]{:S(2)}) collective-permute-start(f32[1,128]{1,0:T(1,128)S(1)} %slice_add_fusion.3), channel_id=1, source_target_pairs={{0,4},{1,5},{2,6},{3,7},{4,8},{5,9},{6,10},{7,11},{8,12},{9,13},{1... | collective-permute-start | bytes 1544 | tf_op jit(solution)/shard_map/ppermute | solution.py:226
  37.1 5.4 %collective-permute-start.8 = (f32[1,128]{1,0:T(1,128)S(1)}, f32[1,128]{1,0:T(1,128)S(1)}, u32[]{:S(2)}, u32[]{:S(2)}) collective-permute-start(f32[1,128]{1,0:T(1,128)S(1)} %add.57), channel_id=1, source_target_pairs={{0,8},{1,9},{2,10},{3,11},{4,12},{5,13},{6,14},{7,15},{8,16},{9,17... | collective-permute-start | bytes 1544 | tf_op jit(solution)/shard_map/ppermute | solution.py:226
  42.4 4.5 %collective-permute-start.9 = (f32[1,128]{1,0:T(1,128)S(1)}, f32[1,128]{1,0:T(1,128)S(1)}, u32[]{:S(2)}, u32[]{:S(2)}) collective-permute-start(f32[1,128]{1,0:T(1,128)S(1)} %add.58), channel_id=1, source_target_pairs={{0,16},{1,17},{2,18},{3,19},{4,20},{5,21},{6,22},{7,23},{8,24},{9,... | collective-permute-start | bytes 1544 | tf_op jit(solution)/shard_map/ppermute | solution.py:226

commit v2 on v1

--- a/solution.py
+++ b/solution.py
@@ -41,9 +41,10 @@
     face_ref,
     rank_ref,
     force_ref,
-    table_ref,
+    sent_ref,
     table_w,
     wide_weight,
+    table_ref,
 ):
     step = pl.program_id(0)
     points = ns_ref.shape[1]
@@ -167,6 +168,19 @@
         table_ref[2 * GROUP : 3 * GROUP, :] = jnp.where(fresh_wins, fresh_low, old_low)
         table_ref[3 * GROUP : 4 * GROUP, :] += (part[8] + part[9]) + part[10]
 
+    @pl.when(step == pl.num_programs(0) - 1)
+    def _():
+        for i in range(PLANES):
+            plane = table_ref[GROUP * i : GROUP * (i + 1), :]
+            sent_ref[OWN_ROWS * i : OWN_ROWS * (i + 1), :] = plane[:OWN_ROWS]
+            at = PLANES * OWN_ROWS + SPILL_ROWS * i
+            sent_ref[at : at + SPILL_ROWS, :] = plane[OWN_ROWS : OWN_ROWS + SPILL_ROWS]
+        for i in range(2):
+            sums = table_ref[5 * GROUP + 8 * i : 5 * GROUP + 8 * (i + 1), :]
+            sent_ref[TOTALS_AT + i : TOTALS_AT + i + 1, :] = jnp.sum(sums, axis=0, keepdims=True)
+        tail = sent_ref.shape[0] - TOTALS_AT - 2
+        sent_ref[TOTALS_AT + 2 :, :] = jnp.zeros((tail, LANES), f32)
+
 
 def local_step(ns, nm, sec, mst, offset, weight, jac, slot, face, rank, live):
     nodes, points = ns.shape
@@ -192,14 +206,15 @@
             tall,
             tall,
         ],
-        out_specs=[wide, whole((6 * GROUP, LANES))],
+        out_specs=[wide, whole((SENT_ROWS, LANES))],
         out_shape=[
             jax.ShapeDtypeStruct((nodes, row_count), jnp.bfloat16),
-            jax.ShapeDtypeStruct((6 * GROUP, LANES), jnp.float32),
+            jax.ShapeDtypeStruct((SENT_ROWS, LANES), jnp.float32),
         ],
         scratch_shapes=[
             pltpu.VMEM((points + GROUP, 2 * nodes + GROUP), jnp.bfloat16),
             pltpu.VMEM((points, LANES), jnp.float32),
+            pltpu.VMEM((6 * GROUP, LANES), jnp.float32),
         ],
     )(
         live,
@@ -216,14 +231,12 @@
     )
 
 
-def sent(value, dom_by, rep_by):
-    doms, reps = lax.axis_size("dom"), lax.axis_size("rep")
-    pairs = [
-        (d * reps + r, (d + dom_by) % doms * reps + (r + rep_by) % reps)
-        for d in range(doms)
-        for r in range(reps)
-    ]
-    return lax.ppermute(value, ("dom", "rep"), pairs)
+OWN_ROWS = SEG_DEV // LANES
+SPILL_ROWS = SPILL // LANES
+PLANES = 4
+TOTALS_AT = PLANES * (OWN_ROWS + SPILL_ROWS)
+SENT_ROWS = -(-(TOTALS_AT + 2) // 8) * 8
+PASSED_ROWS = 16
 
 
 def merge(first, second):
@@ -237,37 +250,66 @@
     )
 
 
-def shards(ns, nm, sec, mst, offset, weight, jac, slot, face, rank, live):
-    doms, reps = lax.axis_size("dom"), lax.axis_size("rep")
-    own_rows, spill_rows = SEG_DEV // LANES, SPILL // LANES
-    force, table = local_step(ns, nm, sec, mst, offset, weight, jac, slot, face, rank, live)
-    planes = [table[GROUP * i : GROUP * (i + 1)] for i in range(4)]
-    totals = jnp.stack([jnp.sum(table[5 * GROUP : 5 * GROUP + 8]), jnp.sum(table[5 * GROUP + 8 :])])
-    totals = jnp.pad(totals, (0, LANES - 2)).reshape(1, LANES)
-    own = jnp.concatenate([plane[:own_rows] for plane in planes] + [totals], axis=0)
-    spill = jnp.concatenate([plane[own_rows : own_rows + spill_rows] for plane in planes], axis=0)
-
-    mates = [own] + [sent(own, 0, k) for k in range(1, reps)]
-    arrivals = [sent(spill, 1, k) for k in range(reps)]
-    split = lambda value, rows: tuple(value[rows * i : rows * (i + 1)] for i in range(4))
-    merged = functools.reduce(merge, [split(value, own_rows) for value in mates])
-    lead = functools.reduce(merge, [split(value, spill_rows) for value in arrivals])
-    lead = merge(tuple(part[:spill_rows] for part in merged), lead)
+def split(value, rows, start=0):
+    return tuple(value[start + rows * i : start + rows * (i + 1)] for i in range(PLANES))
+
+
+def group_kernel(gathered_ref, own_ref, passed_ref):
+    parts = [gathered_ref[i] for i in range(gathered_ref.shape[0])]
+    own = functools.reduce(merge, [split(part, OWN_ROWS) for part in parts])
+    spill_at = PLANES * OWN_ROWS
+    spill = functools.reduce(merge, [split(part, SPILL_ROWS, spill_at) for part in parts])
+    totals = functools.reduce(jnp.add, [part[TOTALS_AT : TOTALS_AT + 2] for part in parts])
+    own_ref[...] = jnp.concatenate(own, axis=0)
+    fill = jnp.zeros((PASSED_ROWS - PLANES * SPILL_ROWS - 2, LANES), jnp.float32)
+    passed = jnp.concatenate(spill + (totals, fill), axis=0)
+    for i in range(passed_ref.shape[0]):
+        passed_ref[i] = passed
+
+
+def final_kernel(before_ref, own_ref, arrived_ref, pen_ref, face_ref, gap_ref, mean_ref):
+    own = split(own_ref[...], OWN_ROWS)
+    spill = split(arrived_ref[before_ref[0]], SPILL_ROWS)
+    lead = merge(tuple(part[:SPILL_ROWS] for part in own), spill)
     pen, high, low, gap = (
-        jnp.concatenate([head, part[spill_rows:]], axis=0) for head, part in zip(lead, merged)
+        jnp.concatenate([head, part[SPILL_ROWS:]], axis=0) for head, part in zip(lead, own)
     )
     empty = pen <= LOWEST_FILL
     key = high.astype(jnp.int32) * 65536 + low.astype(jnp.int32)
-    seg_face = jnp.where(empty, -1, FACE_LIMIT - 1 - (key & (FACE_LIMIT - 1)))
-    seg_pen = jnp.where(empty, 0.0, pen)
-
-    group = functools.reduce(jnp.add, [value[4 * own_rows :] for value in mates])
-    reach = 1
-    while reach < doms:
-        group = group + sent(group, reach, 0)
-        reach *= 2
-    mean_gap = group[0, 0] / group[0, 1]
-    return (force, seg_pen.reshape(-1), seg_face.reshape(-1), gap.reshape(-1), mean_gap)
+    face_ref[...] = jnp.where(empty, -1, FACE_LIMIT - 1 - (key & (FACE_LIMIT - 1)))
+    pen_ref[...] = jnp.where(empty, 0.0, pen)
+    gap_ref[...] = gap
+    at = PLANES * SPILL_ROWS
+    totals = arrived_ref[0, at : at + 2]
+    for i in range(1, arrived_ref.shape[0]):
+        totals += arrived_ref[i, at : at + 2]
+    sums = jnp.sum(totals, axis=1, keepdims=True)
+    mean_ref[...] = jnp.broadcast_to(sums[0:1] / sums[1:2], mean_ref.shape)
+
+
+def shards(ns, nm, sec, mst, offset, weight, jac, slot, face, rank, live):
+    doms = lax.axis_size("dom")
+    f32 = jnp.float32
+    force, table = local_step(ns, nm, sec, mst, offset, weight, jac, slot, face, rank, live)
+    gathered = lax.all_gather(table, "rep")
+    own, passed = pl.pallas_call(
+        group_kernel,
+        out_shape=[
+            jax.ShapeDtypeStruct((PLANES * OWN_ROWS, LANES), f32),
+            jax.ShapeDtypeStruct((doms, PASSED_ROWS, LANES), f32),
+        ],
+    )(gathered)
+    arrived = lax.all_to_all(passed, "dom", 0, 0)
+    before = (lax.axis_index("dom") + doms - 1) % doms
+    plane = lambda dtype: jax.ShapeDtypeStruct((OWN_ROWS, LANES), dtype)
+    vmem = pl.BlockSpec(memory_space=pltpu.VMEM)
+    pen, chosen, gap, mean = pl.pallas_call(
+        final_kernel,
+        in_specs=[pl.BlockSpec(memory_space=pltpu.SMEM), vmem, vmem],
+        out_specs=[vmem] * 4,
+        out_shape=[plane(f32), plane(jnp.int32), plane(f32), jax.ShapeDtypeStruct((1, 1), f32)],
+    )(before.reshape(1), own, arrived)
+    return (force, pen.reshape(-1), chosen.reshape(-1), gap.reshape(-1), mean.reshape(()))
 
 
 def solution(mesh):

time: 50.3 us -> 37.8 us (0.75)
  blocking collectives: 0 us -> 8.25 us
  starting transfers between devices: 12.7 us -> 5.84 us
  waiting for transfers between devices: 13.3 us -> 6.9 us
  other arithmetic: 5.26 us -> 0 us
  Pallas kernels: 11.4 us -> 14.5 us
  local copies, waits for them, and re-layouts: 3.42 us -> 0.62 us
  between operations: 3.83 us -> 1.29 us
    ppermute x10 -> x0, waiting for transfers between devices: 13.3 us -> none  [sent(): return lax.ppermute(value, ('dom', 'rep'), pairs)]
    ppermute x10 -> x0, starting transfers between devices: 12.7 us -> none  [sent(): return lax.ppermute(value, ('dom', 'rep'), pairs)]
    all_gather x0 -> x1, blocking collectives: none -> 8.25 us  [shards(): gathered = lax.all_gather(table, 'rep')]
    all_to_all x0 -> x1, waiting for transfers between devices: none -> 6.9 us  [shards(): arrived = lax.all_to_all(passed, 'dom', 0, 0)]
    all_to_all x0 -> x1, starting transfers between devices: none -> 5.84 us  [shards(): arrived = lax.all_to_all(passed, 'dom', 0, 0)]
    pallas_call x0 -> x2, Pallas kernels: none -> 3.02 us  [the longest x1 1.55 us: shards(): pl.pallas_call(group_kernel, out_shape=[jax.ShapeDtypeStruct((PLANES * OW...]
    reshape x2 -> x0, other arithmetic: 1.97 us -> none  [the longest x1 1.37 us: shards(): totals = jnp.pad(totals, (0, LANES - 2)).reshape(1, LANES)]
    unnamed x5 -> x2, local copies, waits for them, and re-layouts: 2.05 us -> 0.62 us
  transfers between devices with their start and end apart: 10 -> 1, of which waited for: 4 -> 1; matrix products, arithmetic and copies ran while one was open for 15% -> 0% of each run, Pallas kernels for 0% -> 0%
where the time goes in v2:
time: 37.8 us; the launch traced here: 37.4 us
  Pallas kernels  14.5 us (38%)
  blocking collectives  8.25 us (22%)
  waiting for transfers between devices  6.9 us (18%)
  starting transfers between devices  5.84 us (15%)
  between operations  1.29 us (3%)
  local copies, waits for them, and re-layouts  0.62 us (2%)
    pallas_call x1, Pallas kernels, local_step(): pl.pallas_call(local_kernel, grid=(row_count // rows,), in_specs=[pl.Bloc...  11.5 us
    all_gather x1, blocking collectives, shards(): gathered = lax.all_gather(table, 'rep')  8.25 us
    all_to_all x1, waiting for transfers between devices, shards(): arrived = lax.all_to_all(passed, 'dom', 0, 0)  6.9 us
    all_to_all x1, starting transfers between devices, shards(): arrived = lax.all_to_all(passed, 'dom', 0, 0)  5.84 us
    pallas_call x1, Pallas kernels, shards(): pl.pallas_call(group_kernel, out_shape=[jax.ShapeDtypeStruct((PLANES * OW...  1.55 us
    pallas_call x1, Pallas kernels, shards(): pl.pallas_call(final_kernel, in_specs=[pl.BlockSpec(memory_space=pltpu.SM...  1.47 us
  transfers between devices with their start and end apart: 1, of which 1 were waited for; matrix products, arithmetic and copies ran while one was open for 0% of the time, Pallas kernels for 0%

profile of v2, /device:TPU:0, one launch (start us, length us, event | category | flops | bytes accessed | tf_op | source)
XLA Modules:
  0.0 37.4 jit_solution(15354571833927345851)
XLA Ops:
  1.3 11.5 %shard_map.146 = (bf16[64,8192]{1,0:T(8,128)(2,1)}, f32[48,128]{1,0:T(8,128)}) custom-call(s32[1]{0:T(128)S(6)} %copy.16.live_ref, bf16[64,256]{1,0:T(8,128)(2,1)} %ns_ref.1, bf16[64,256]{1,0:T(8,128)(2,1)} %nm_ref.1, f32[1,256]{1,0:T(1,128)} %bitcast.18, bf16[64,8192]{1,0:T(8,128)(2,1)} %sec_ref.1, bf16[64,8192]{1,0:T(8,128)(2,1)} %mst_ref.1, ...), custom_call_target="tpu_custom_call" | custom-call | tf_op jit(solution)/shard_map/pallas_call | solution.py:193
  12.8 8.2 %all-gather = f32[192,128]{1,0:T(8,128)} all-gather(f32[48,128]{1,0:T(8,128)} %get-tuple-element.14), channel_id=2, replica_groups=mesh['dom'=8,'rep'=4] {'rep'}, dimensions={0}, use_global_device_ids=true | all-gather | bytes 122880 | tf_op jit(solution)/shard_map/all_gather | solution.py:294
  21.1 1.5 %shard_map.147 = (f32[32,128]{1,0:T(8,128)}, f32[8,16,128]{2,1,0:T(8,128)}) custom-call(f32[4,48,128]{2,1,0:T(8,128)} %bitcast.12), custom_call_target="tpu_custom_call" | custom-call | tf_op jit(solution)/shard_map/pallas_call | solution.py:295
  22.6 5.8 %all-to-all-start = ((f32[8,16,128]{2,1,0:T(8,128)}), f32[8,16,128]{2,1,0:T(8,128)S(1)}, u32[]{:S(2)}, u32[]{:S(2)}) async-start(f32[8,16,128]{2,1,0:T(8,128)} %get-tuple-element.16), calls=%async_computation | async-start | bytes 131072 | tf_op jit(solution)/shard_map/all_to_all | solution.py:302
  28.4 6.9 %all-to-all-done.arrived_ref = f32[8,16,128]{2,1,0:T(8,128)S(1)} async-done(((f32[8,16,128]{2,1,0:T(8,128)}), f32[8,16,128]{2,1,0:T(8,128)S(1)}, u32[]{:S(2)}, u32[]{:S(2)}) %all-to-all-start) | async-done | bytes 65568 | tf_op jit(solution)/shard_map/all_to_all | solution.py:302
  35.3 0.0 copy-start
  35.3 0.6 %copy-done = f32[8,16,128]{2,1,0:T(8,128)} copy-done((f32[8,16,128]{2,1,0:T(8,128)}, f32[8,16,128]{2,1,0:T(8,128)S(1)}, u32[]{:S(2)}) %copy-start) | copy-done | bytes 65560
  36.0 1.5 %shard_map.148 = (f32[8,128]{1,0:T(8,128)}, s32[8,128]{1,0:T(8,128)}, f32[8,128]{1,0:T(8,128)}, f32[1,1]{1,0:T(1,128)}) custom-call(s32[1]{0:T(128)} %bitcast.6.before_ref, f32[32,128]{1,0:T(8,128)} %get-tuple-element.15.own_ref, f32[8,16,128]{2,1,0:T(8,128)} %copy-done), custom_call_target="tpu_custom_call" | custom-call | tf_op jit(solution)/shard_map/pallas_call | solution.py:306
Async XLA Ops:
  22.6 12.7 %all-to-all-start = ((f32[8,16,128]{2,1,0:T(8,128)}), f32[8,16,128]{2,1,0:T(8,128)S(1)}, u32[]{:S(2)}, u32[]{:S(2)}) async-start(f32[8,16,128]{2,1,0:T(8,128)} %get-tuple-element.16), calls=%async_computation | async-start | bytes 131072 | tf_op jit(solution)/shard_map/all_to_all | solution.py:302
  35.3 0.6 %copy-start = (f32[8,16,128]{2,1,0:T(8,128)}, f32[8,16,128]{2,1,0:T(8,128)S(1)}, u32[]{:S(2)}) copy-start(f32[8,16,128]{2,1,0:T(8,128)S(1)} %all-to-all-done.arrived_ref) | copy-start | bytes 196612

commit v3 on v2

--- a/solution.py
+++ b/solution.py
@@ -28,7 +28,51 @@
     return parts
 
 
-def local_kernel(
+def as_row(value):
+    return jnp.concatenate([value[b : b + 1, :] for b in range(value.shape[0])], axis=1)
+
+
+def as_block(value):
+    return jnp.concatenate(
+        [value[:, LANES * b : LANES * (b + 1)] for b in range(value.shape[1] // LANES)], axis=0
+    )
+
+
+def stacked_inputs(sec_ref, mst_ref, offset_ref):
+    off = [as_row(part) for part in pieces_of(offset_ref[...], 3)]
+    sub = lax.broadcasted_iota(jnp.int32, (GROUP, sec_ref.shape[1]), 0)
+    rest = jnp.where(sub == 0, off[0], jnp.where(sub == 1, off[1], jnp.where(sub == 2, off[2], 0.0)))
+    return jnp.concatenate([sec_ref[...], mst_ref[...], rest.astype(jnp.bfloat16)], axis=0)
+
+
+def live_of(shape, live_count):
+    row_ids = (
+        pl.program_id(0) * (shape[0] * shape[1])
+        + shape[1] * lax.broadcasted_iota(jnp.int32, shape, 0)
+        + lax.broadcasted_iota(jnp.int32, shape, 1)
+    )
+    return row_ids < live_count
+
+
+def force_kernel(
+    live_ref, ns_ref, table_ref, weight_ref, sec_ref, mst_ref, offset_ref, jac_ref, force_ref
+):
+    points = ns_ref.shape[1]
+    f32 = jnp.float32
+    field = jnp.dot(
+        table_ref[0:points, :], stacked_inputs(sec_ref, mst_ref, offset_ref), preferred_element_type=f32
+    )
+    weights = weight_ref[...]
+    loads = [
+        (jnp.minimum(field[:, at : at + LANES], 0.0) * weights).astype(jnp.bfloat16)
+        for at in range(0, field.shape[1], LANES)
+    ]
+    force = jnp.dot(ns_ref[...], jnp.concatenate(loads, axis=1), preferred_element_type=f32)
+    scale = jnp.where(live_of(jac_ref.shape, live_ref[0]), jac_ref[...] * -PENALTY, 0.0)
+    force_ref[...] = (force * as_row(scale)).astype(jnp.bfloat16)
+
+
+def stats_kernel(
     live_ref,
     ns_ref,
     nm_ref,
@@ -40,7 +84,6 @@
     slot_ref,
     face_ref,
     rank_ref,
-    force_ref,
     sent_ref,
     table_w,
     wide_weight,
@@ -78,64 +121,36 @@
         table_ref[0:GROUP, :] = jnp.full((GROUP, LANES), LOWEST_FILL, f32)
         table_ref[GROUP:, :] = jnp.zeros((table_ref.shape[0] - GROUP, LANES), f32)
 
-    live_count = live_ref[0]
-    row_ids = (
-        step * rows
-        + LANES * lax.broadcasted_iota(i32, (blocks, LANES), 0)
-        + lax.broadcasted_iota(i32, (blocks, LANES), 1)
-    )
-    live = row_ids < live_count
+    live = live_of(jac_ref.shape, live_ref[0])
     jac = jac_ref[...]
 
-    def as_row(value):
-        return jnp.concatenate([value[b : b + 1, :] for b in range(blocks)], axis=1)
-
-    def as_block(value):
-        return jnp.concatenate([value[:, LANES * b : LANES * (b + 1)] for b in range(blocks)], axis=0)
-
-    off = pieces_of(offset_ref[...], 3)
-    sub = lax.broadcasted_iota(i32, (GROUP, rows), 0)
-    off_rows = jnp.where(
-        sub == 0, as_row(off[0]), jnp.where(sub == 1, as_row(off[1]), jnp.where(sub == 2, as_row(off[2]), 0.0))
-    ).astype(bf16)
-    stacked = jnp.concatenate([sec_ref[...], mst_ref[...], off_rows], axis=0)
-    gaps = jnp.dot(table_w[...], stacked, preferred_element_type=f32)
-    field = gaps[0:points, :]
-    pen = as_block(-jnp.min(field, axis=0, keepdims=True))
-    weighted = as_block(gaps[points : points + 1, :] + gaps[points + 1 : points + 2, :] + gaps[points + 2 : points + 3, :])
-
-    weights = wide_weight[...]
-    scale = jnp.where(live, jac * -PENALTY, 0.0)
-    loads = jnp.concatenate(
-        [
-            (jnp.minimum(field[:, LANES * b : LANES * (b + 1)], 0.0) * weights).astype(bf16)
-            for b in range(blocks)
-        ],
-        axis=1,
-    )
-    force = jnp.dot(ns_ref[...], loads, preferred_element_type=f32)
-    force_ref[...] = (force * as_row(scale)).astype(bf16)
+    gaps = jnp.dot(table_w[...], stacked_inputs(sec_ref, mst_ref, offset_ref), preferred_element_type=f32)
+    pen = as_block(-jnp.min(gaps[0:points, :], axis=0, keepdims=True))
+    weighted = as_block(
+        gaps[points : points + 1, :] + gaps[points + 1 : points + 2, :] + gaps[points + 2 : points + 3, :]
+    )
 
     row_gap = jnp.where(live, jac * weighted, 0.0)
     row_area = jnp.where(live, jac * jnp.sum(weight_ref[...], axis=1, keepdims=True), 0.0)
-    table_ref[5 * GROUP : 5 * GROUP + blocks, :] += row_gap
-    table_ref[5 * GROUP + 8 : 5 * GROUP + 8 + blocks, :] += row_area
+    table_ref[4 * GROUP : 4 * GROUP + blocks, :] += row_gap
+    table_ref[5 * GROUP : 5 * GROUP + blocks, :] += row_area
 
     slot = jnp.where(live, slot_ref[...], (GROUP - 1) * LANES)
     key = ((rank_ref[...] - 2) << 30) + (FACE_LIMIT - 1 - face_ref[...])
     gap_parts = pieces_of(row_gap, 3)
     slot_t, pen_t, key_t = jnp.transpose(slot), jnp.transpose(pen), jnp.transpose(key)
-    sub = lax.broadcasted_iota(i32, (LANES, LANES), 0)
+    place = lax.broadcasted_iota(i32, (LANES, LANES), 0).astype(f32)
     lane = lax.broadcasted_iota(i32, (LANES, LANES), 1)
     group_id = lax.broadcasted_iota(i32, (GROUP, LANES), 0)
+    old_pen, old_high, old_low, old_gap = (table_ref[GROUP * i : GROUP * (i + 1), :] for i in range(PLANES))
     for b in range(blocks):
         slot_col = jnp.broadcast_to(slot_t[:, b : b + 1], (LANES, LANES))
         slot_row = slot[b : b + 1, :]
         same = slot_col == slot_row
         top_pen = jnp.max(jnp.where(same, pen_t[:, b : b + 1], LOWEST_FILL), axis=0, keepdims=True)
         top_key = jnp.max(jnp.where(same, key_t[:, b : b + 1], NO_KEY), axis=0, keepdims=True)
-        last = jnp.max(jnp.where(same, sub, -1), axis=0, keepdims=True)
-        speaks = last == lax.broadcasted_iota(i32, (1, LANES), 1)
+        last = jnp.max(jnp.where(same, place, -1.0), axis=0, keepdims=True)
+        speaks = last == lax.broadcasted_iota(i32, (1, LANES), 1).astype(f32)
         home = (slot_row >> 7) == group_id
         spoken = home & speaks
         one_hot = jnp.where((slot_col & (LANES - 1)) == lane, 1.0, 0.0).astype(bf16)
@@ -155,18 +170,17 @@
         fresh_pen = jnp.where(there, (part[0] + part[1]) + part[2], LOWEST_FILL)
         fresh_high = part[6] * 256.0 + part[5]
         fresh_low = part[4] * 256.0 + part[3]
-        old_pen = table_ref[0:GROUP, :]
-        old_high = table_ref[GROUP : 2 * GROUP, :]
-        old_low = table_ref[2 * GROUP : 3 * GROUP, :]
         fresh_wins = there & (
             (old_pen == LOWEST_FILL)
             | (fresh_high > old_high)
             | ((fresh_high == old_high) & (fresh_low > old_low))
         )
-        table_ref[0:GROUP, :] = jnp.maximum(old_pen, fresh_pen)
-        table_ref[GROUP : 2 * GROUP, :] = jnp.where(fresh_wins, fresh_high, old_high)
-        table_ref[2 * GROUP : 3 * GROUP, :] = jnp.where(fresh_wins, fresh_low, old_low)
-        table_ref[3 * GROUP : 4 * GROUP, :] += (part[8] + part[9]) + part[10]
+        old_pen = jnp.maximum(old_pen, fresh_pen)
+        old_high = jnp.where(fresh_wins, fresh_high, old_high)
+        old_low = jnp.where(fresh_wins, fresh_low, old_low)
+        old_gap += (part[8] + part[9]) + part[10]
+    for i, plane in enumerate((old_pen, old_high, old_low, old_gap)):
+        table_ref[GROUP * i : GROUP * (i + 1), :] = plane
 
     @pl.when(step == pl.num_programs(0) - 1)
     def _():
@@ -176,59 +190,61 @@
             at = PLANES * OWN_ROWS + SPILL_ROWS * i
             sent_ref[at : at + SPILL_ROWS, :] = plane[OWN_ROWS : OWN_ROWS + SPILL_ROWS]
         for i in range(2):
-            sums = table_ref[5 * GROUP + 8 * i : 5 * GROUP + 8 * (i + 1), :]
+            sums = table_ref[(PLANES + i) * GROUP : (PLANES + i + 1) * GROUP, :]
             sent_ref[TOTALS_AT + i : TOTALS_AT + i + 1, :] = jnp.sum(sums, axis=0, keepdims=True)
         tail = sent_ref.shape[0] - TOTALS_AT - 2
         sent_ref[TOTALS_AT + 2 :, :] = jnp.zeros((tail, LANES), f32)
 
 
-def local_step(ns, nm, sec, mst, offset, weight, jac, slot, face, rank, live):
-    nodes, points = ns.shape
-    row_count = sec.shape[1]
-    rows = min(row_count, 1024)
-    folded = lambda value: value.reshape(row_count // LANES, LANES)
-    whole = lambda shape: pl.BlockSpec(shape, lambda i: (0, 0))
+def specs_of(ns, sec):
+    nodes, row_count = ns.shape[0], sec.shape[1]
+    rows = min(row_count, GROUP * LANES)
     wide = pl.BlockSpec((nodes, rows), lambda i: (0, i))
     tall = pl.BlockSpec((rows // LANES, LANES), lambda i: (i, 0))
+    return (row_count // rows,), wide, tall
+
+
+def whole(shape):
+    return pl.BlockSpec(shape, lambda i: (0, 0))
+
+
+def stats_of(ns, nm, sec, mst, offset, weight, jac, slot, face, rank, live):
+    nodes, points = ns.shape
+    grid, wide, tall = specs_of(ns, sec)
+    shapes = [
+        ((SENT_ROWS, LANES), jnp.float32),
+        ((points + GROUP, 2 * nodes + GROUP), jnp.bfloat16),
+        ((points, LANES), jnp.float32),
+    ]
     return pl.pallas_call(
-        local_kernel,
-        grid=(row_count // rows,),
-        in_specs=[
-            pl.BlockSpec(memory_space=pltpu.SMEM),
-            whole((nodes, points)),
-            whole((nodes, points)),
-            whole((1, points)),
-            wide,
-            wide,
-            tall,
-            tall,
-            tall,
-            tall,
-            tall,
-        ],
-        out_specs=[wide, whole((SENT_ROWS, LANES))],
-        out_shape=[
-            jax.ShapeDtypeStruct((nodes, row_count), jnp.bfloat16),
-            jax.ShapeDtypeStruct((SENT_ROWS, LANES), jnp.float32),
-        ],
-        scratch_shapes=[
-            pltpu.VMEM((points + GROUP, 2 * nodes + GROUP), jnp.bfloat16),
-            pltpu.VMEM((points, LANES), jnp.float32),
-            pltpu.VMEM((6 * GROUP, LANES), jnp.float32),
-        ],
-    )(
-        live,
-        ns,
-        nm,
-        weight.reshape(1, points),
-        sec,
-        mst,
-        folded(offset),
-        folded(jac),
-        folded(slot),
-        folded(face),
-        folded(rank),
-    )
+        stats_kernel,
+        grid=grid,
+        in_specs=[pl.BlockSpec(memory_space=pltpu.SMEM)]
+        + [whole(ns.shape)] * 2
+        + [whole((1, points))]
+        + [wide] * 2
+        + [tall] * 5,
+        out_specs=[whole(shape) for shape, _ in shapes],
+        out_shape=[jax.ShapeDtypeStruct(shape, dtype) for shape, dtype in shapes],
+        scratch_shapes=[pltpu.VMEM((6 * GROUP, LANES), jnp.float32)],
+    )(live, ns, nm, weight.reshape(1, points), sec, mst, offset, jac, slot, face, rank)
+
+
+def force_of(ns, table, weight, sec, mst, offset, jac, live):
+    grid, wide, tall = specs_of(ns, sec)
+    nodes, points = ns.shape
+    work = 2 * sec.shape[1] * points * (3 * nodes + GROUP)
+    return pl.pallas_call(
+        force_kernel,
+        grid=grid,
+        in_specs=[pl.BlockSpec(memory_space=pltpu.SMEM)]
+        + [whole(ns.shape), whole(table.shape), whole(weight.shape)]
+        + [wide] * 2
+        + [tall] * 2,
+        out_specs=wide,
+        out_shape=jax.ShapeDtypeStruct(sec.shape, jnp.bfloat16),
+        cost_estimate=pl.CostEstimate(flops=20 * work, bytes_accessed=6 * sec.size, transcendentals=0),
+    )(live, ns, table, weight, sec, mst, offset, jac)
 
 
 OWN_ROWS = SEG_DEV // LANES
@@ -290,7 +306,12 @@
 def shards(ns, nm, sec, mst, offset, weight, jac, slot, face, rank, live):
     doms = lax.axis_size("dom")
     f32 = jnp.float32
-    force, table = local_step(ns, nm, sec, mst, offset, weight, jac, slot, face, rank, live)
+    offset, jac, slot, face, rank = (
+        value.reshape(-1, LANES) for value in (offset, jac, slot, face, rank)
+    )
+    table, table_w, wide_weight = stats_of(
+        ns, nm, sec, mst, offset, weight, jac, slot, face, rank, live
+    )
     gathered = lax.all_gather(table, "rep")
     own, passed = pl.pallas_call(
         group_kernel,
@@ -300,6 +321,7 @@
         ],
     )(gathered)
     arrived = lax.all_to_all(passed, "dom", 0, 0)
+    force = force_of(ns, table_w, wide_weight, sec, mst, offset, jac, live)
     before = (lax.axis_index("dom") + doms - 1) % doms
     plane = lambda dtype: jax.ShapeDtypeStruct((OWN_ROWS, LANES), dtype)
     vmem = pl.BlockSpec(memory_space=pltpu.VMEM)

time: 37.8 us -> 36 us (0.952)
  waiting for transfers between devices: 6.9 us -> 1.94 us
  Pallas kernels: 14.5 us -> 17.6 us
    all_to_all x1, waiting for transfers between devices: 6.9 us -> 1.94 us  [shards(): arrived = lax.all_to_all(passed, 'dom', 0, 0)]
    pallas_call x1 -> x2, Pallas kernels: 11.5 us -> 14.6 us  [the longest x1 9.66 us: stats_of(): pl.pallas_call(stats_kernel, grid=grid, in_specs=[pl.BlockSpec(memory_spa...]
  transfers between devices with their start and end apart: 1 -> 1, of which waited for: 1 -> 1; matrix products, arithmetic and copies ran while one was open for 0% -> 0% of each run, Pallas kernels for 0% -> 14%
where the time goes in v3:
time: 36 us; the launch traced here: 35.6 us
  Pallas kernels  17.6 us (49%)
  blocking collectives  8.24 us (23%)
  starting transfers between devices  5.84 us (16%)
  waiting for transfers between devices  1.94 us (5%)
  between operations  1.28 us (4%)
  local copies, waits for them, and re-layouts  0.62 us (2%)
    pallas_call x1, Pallas kernels, stats_of(): pl.pallas_call(stats_kernel, grid=grid, in_specs=[pl.BlockSpec(memory_spa...  9.66 us
    all_gather x1, blocking collectives, shards(): gathered = lax.all_gather(table, 'rep')  8.24 us
    all_to_all x1, starting transfers between devices, shards(): arrived = lax.all_to_all(passed, 'dom', 0, 0)  5.84 us
    pallas_call x1, Pallas kernels, force_of(): pl.pallas_call(force_kernel, grid=grid, in_specs=[pl.BlockSpec(memory_spa...  4.96 us
    all_to_all x1, waiting for transfers between devices, shards(): arrived = lax.all_to_all(passed, 'dom', 0, 0)  1.94 us
    pallas_call x1, Pallas kernels, shards(): pl.pallas_call(group_kernel, out_shape=[jax.ShapeDtypeStruct((PLANES * OW...  1.55 us
    pallas_call x1, Pallas kernels, shards(): pl.pallas_call(final_kernel, in_specs=[pl.BlockSpec(memory_space=pltpu.SM...  1.47 us
  transfers between devices with their start and end apart: 1, of which 1 were waited for; matrix products, arithmetic and copies ran while one was open for 0% of the time, Pallas kernels for 14%

profile of v3, /device:TPU:0, one launch (start us, length us, event | category | flops | bytes accessed | tf_op | source)
XLA Modules:
  0.0 35.6 jit_solution(13031355242805396521)
XLA Ops:
  1.3 9.7 %shard_map.146 = (f32[48,128]{1,0:T(8,128)}, bf16[272,144]{1,0:T(8,128)(2,1)}, f32[256,128]{1,0:T(8,128)}) custom-call(s32[1]{0:T(128)S(6)} %copy.16.live_ref, bf16[64,256]{1,0:T(8,128)(2,1)} %ns_ref.3, bf16[64,256]{1,0:T(8,128)(2,1)} %nm_ref.1, f32[1,256]{1,0:T(1,128)} %bitcast.20, bf16[64,8192]{1,0:T(8,128)(2,1)} %sec_ref.3, bf16[64,8192]{1,0:T(8,128)(2,1)} %mst_ref.3, ...), custom_call_target="tpu_custom_call" | custom-call | tf_op jit(solution)/shard_map/pallas_call | solution.py:219
  10.9 8.2 %all-gather = f32[192,128]{1,0:T(8,128)} all-gather(f32[48,128]{1,0:T(8,128)} %get-tuple-element.16), channel_id=2, replica_groups=mesh['dom'=8,'rep'=4] {'rep'}, dimensions={0}, use_global_device_ids=true | all-gather | bytes 122880 | tf_op jit(solution)/shard_map/all_gather | solution.py:315
  19.2 1.6 %shard_map.148 = (f32[32,128]{1,0:T(8,128)}, f32[8,16,128]{2,1,0:T(8,128)}) custom-call(f32[4,48,128]{2,1,0:T(8,128)} %bitcast.12), custom_call_target="tpu_custom_call" | custom-call | tf_op jit(solution)/shard_map/pallas_call | solution.py:316
  20.7 5.8 %all-to-all-start = ((f32[8,16,128]{2,1,0:T(8,128)}), f32[8,16,128]{2,1,0:T(8,128)S(1)}, u32[]{:S(2)}, u32[]{:S(2)}) async-start(f32[8,16,128]{2,1,0:T(8,128)} %get-tuple-element.18), calls=%async_computation | async-start | bytes 131072 | tf_op jit(solution)/shard_map/all_to_all | solution.py:323
  26.6 5.0 %shard_map.147 = bf16[64,8192]{1,0:T(8,128)(2,1)} custom-call(s32[1]{0:T(128)S(6)} %copy.16.live_ref, bf16[64,256]{1,0:T(8,128)(2,1)} %ns_ref.3, bf16[272,144]{1,0:T(8,128)(2,1)} %get-tuple-element.14.table_ref, f32[256,128]{1,0:T(8,128)} %get-tuple-element.15.weight_ref, bf16[64,8192]{1,0:T(8,128)(2,1)} %sec_ref.3, bf16[64,8192]{1,0:T(8,128)(2,1)} %mst_ref.3, ...), custom_call_target="tpu_custom_call" | custom-call | flops 17448304640 | bytes 3145728 | tf_op jit(solution)/shard_map/pallas_call | solution.py:237
  31.5 1.9 %all-to-all-done.arrived_ref = f32[8,16,128]{2,1,0:T(8,128)S(1)} async-done(((f32[8,16,128]{2,1,0:T(8,128)}), f32[8,16,128]{2,1,0:T(8,128)S(1)}, u32[]{:S(2)}, u32[]{:S(2)}) %all-to-all-start) | async-done | bytes 65568 | tf_op jit(solution)/shard_map/all_to_all | solution.py:323
  33.5 0.0 copy-start
  33.5 0.6 %copy-done = f32[8,16,128]{2,1,0:T(8,128)} copy-done((f32[8,16,128]{2,1,0:T(8,128)}, f32[8,16,128]{2,1,0:T(8,128)S(1)}, u32[]{:S(2)}) %copy-start) | copy-done | bytes 65560
  34.1 1.5 %shard_map.149 = (f32[8,128]{1,0:T(8,128)}, s32[8,128]{1,0:T(8,128)}, f32[8,128]{1,0:T(8,128)}, f32[1,1]{1,0:T(1,128)}) custom-call(s32[1]{0:T(128)} %bitcast.6.before_ref, f32[32,128]{1,0:T(8,128)} %get-tuple-element.17.own_ref, f32[8,16,128]{2,1,0:T(8,128)} %copy-done), custom_call_target="tpu_custom_call" | custom-call | tf_op jit(solution)/shard_map/pallas_call | solution.py:328
Async XLA Ops:
  20.7 12.7 %all-to-all-start = ((f32[8,16,128]{2,1,0:T(8,128)}), f32[8,16,128]{2,1,0:T(8,128)S(1)}, u32[]{:S(2)}, u32[]{:S(2)}) async-start(f32[8,16,128]{2,1,0:T(8,128)} %get-tuple-element.18), calls=%async_computation | async-start | bytes 131072 | tf_op jit(solution)/shard_map/all_to_all | solution.py:323
  33.5 0.6 %copy-start = (f32[8,16,128]{2,1,0:T(8,128)}, f32[8,16,128]{2,1,0:T(8,128)S(1)}, u32[]{:S(2)}) copy-start(f32[8,16,128]{2,1,0:T(8,128)S(1)} %all-to-all-done.arrived_ref) | copy-start | bytes 196612

commit v4 on v3

--- a/solution.py
+++ b/solution.py
@@ -270,12 +270,20 @@
     return tuple(value[start + rows * i : start + rows * (i + 1)] for i in range(PLANES))
 
 
-def group_kernel(gathered_ref, own_ref, passed_ref):
-    parts = [gathered_ref[i] for i in range(gathered_ref.shape[0])]
-    own = functools.reduce(merge, [split(part, OWN_ROWS) for part in parts])
+def in_pairs(join, parts):
+    while len(parts) > 1 and len(parts) % 2 == 0:
+        half = len(parts) // 2
+        parts = [join(parts[i], parts[i + half]) for i in range(half)]
+    return functools.reduce(join, parts)
+
+
+def group_kernel(*refs):
+    own_ref, passed_ref = refs[-2:]
+    parts = [ref[...] for ref in refs[:-2]]
+    own = in_pairs(merge, [split(part, OWN_ROWS) for part in parts])
     spill_at = PLANES * OWN_ROWS
-    spill = functools.reduce(merge, [split(part, SPILL_ROWS, spill_at) for part in parts])
-    totals = functools.reduce(jnp.add, [part[TOTALS_AT : TOTALS_AT + 2] for part in parts])
+    spill = in_pairs(merge, [split(part, SPILL_ROWS, spill_at) for part in parts])
+    totals = in_pairs(jnp.add, [part[TOTALS_AT : TOTALS_AT + 2] for part in parts])
     own_ref[...] = jnp.concatenate(own, axis=0)
     fill = jnp.zeros((PASSED_ROWS - PLANES * SPILL_ROWS - 2, LANES), jnp.float32)
     passed = jnp.concatenate(spill + (totals, fill), axis=0)
@@ -312,14 +320,17 @@
     table, table_w, wide_weight = stats_of(
         ns, nm, sec, mst, offset, weight, jac, slot, face, rank, live
     )
-    gathered = lax.all_gather(table, "rep")
+    reps = lax.axis_size("rep")
+    mates = [table] + [
+        lax.ppermute(table, "rep", [(i, (i + k) % reps) for i in range(reps)]) for k in range(1, reps)
+    ]
     own, passed = pl.pallas_call(
         group_kernel,
         out_shape=[
             jax.ShapeDtypeStruct((PLANES * OWN_ROWS, LANES), f32),
             jax.ShapeDtypeStruct((doms, PASSED_ROWS, LANES), f32),
         ],
-    )(gathered)
+    )(*mates)
     arrived = lax.all_to_all(passed, "dom", 0, 0)
     force = force_of(ns, table_w, wide_weight, sec, mst, offset, jac, live)
     before = (lax.axis_index("dom") + doms - 1) % doms

time: 36 us -> 35.5 us (0.986)
  blocking collectives: 8.24 us -> 0 us
  waiting for transfers between devices: 1.94 us -> 5.46 us
  starting transfers between devices: 5.84 us -> 9.03 us
  local copies, waits for them, and re-layouts: 0.62 us -> 1.77 us
    all_gather x1 -> x0, blocking collectives: 8.24 us -> none  [shards(): gathered = lax.all_gather(table, 'rep')]
    ppermute x0 -> x3, waiting for transfers between devices: none -> 3.51 us  [shards(): lax.ppermute(table, 'rep', [(i, (i + k) % reps) for i in range(reps)])]
    ppermute x0 -> x3, starting transfers between devices: none -> 3.19 us  [shards(): lax.ppermute(table, 'rep', [(i, (i + k) % reps) for i in range(reps)])]
    unnamed x2 -> x8, local copies, waits for them, and re-layouts: 0.62 us -> 1.77 us
  transfers between devices with their start and end apart: 1 -> 4, of which waited for: 1 -> 4; matrix products, arithmetic and copies ran while one was open for 0% -> 0% of each run, Pallas kernels for 14% -> 14%
where the time goes in v4:
time: 35.5 us; the launch traced here: 35.1 us
  Pallas kernels  17.5 us (49%)
  starting transfers between devices  9.03 us (25%)
  waiting for transfers between devices  5.46 us (15%)
  local copies, waits for them, and re-layouts  1.77 us (5%)
  between operations  1.29 us (4%)
    pallas_call x1, Pallas kernels, stats_of(): pl.pallas_call(stats_kernel, grid=grid, in_specs=[pl.BlockSpec(memory_spa...  9.66 us
    all_to_all x1, starting transfers between devices, shards(): arrived = lax.all_to_all(passed, 'dom', 0, 0)  5.83 us
    pallas_call x1, Pallas kernels, force_of(): pl.pallas_call(force_kernel, grid=grid, in_specs=[pl.BlockSpec(memory_spa...  4.95 us
    ppermute x3, waiting for transfers between devices, shards(): lax.ppermute(table, 'rep', [(i, (i + k) % reps) for i in range(reps)])  3.51 us
    ppermute x3, starting transfers between devices, shards(): lax.ppermute(table, 'rep', [(i, (i + k) % reps) for i in range(reps)])  3.19 us
    all_to_all x1, waiting for transfers between devices, shards(): arrived = lax.all_to_all(passed, 'dom', 0, 0)  1.96 us
    unnamed x8, local copies, waits for them, and re-layouts  1.77 us
    pallas_call x1, Pallas kernels, shards(): pl.pallas_call(final_kernel, in_specs=[pl.BlockSpec(memory_space=pltpu.SM...  1.47 us
  transfers between devices with their start and end apart: 4, of which 4 were waited for; matrix products, arithmetic and copies ran while one was open for 0% of the time, Pallas kernels for 14%

profile of v4, /device:TPU:0, one launch (start us, length us, event | category | flops | bytes accessed | tf_op | source)
XLA Modules:
  0.0 35.1 jit_solution(13423511643345934847)
XLA Ops:
  1.3 9.7 %shard_map.146 = (f32[48,128]{1,0:T(8,128)}, bf16[272,144]{1,0:T(8,128)(2,1)}, f32[256,128]{1,0:T(8,128)}) custom-call(s32[1]{0:T(128)S(6)} %copy.16.live_ref, bf16[64,256]{1,0:T(8,128)(2,1)} %ns_ref.3, bf16[64,256]{1,0:T(8,128)(2,1)} %nm_ref.1, f32[1,256]{1,0:T(1,128)} %bitcast.18, bf16[64,8192]{1,0:T(8,128)(2,1)} %sec_ref.3, bf16[64,8192]{1,0:T(8,128)(2,1)} %mst_ref.3, ...), custom_call_target="tpu_custom_call" | custom-call | tf_op jit(solution)/shard_map/pallas_call | solution.py:219
  10.9 2.4 %collective-permute-start.2 = (f32[48,128]{1,0:T(8,128)}, f32[48,128]{1,0:T(8,128)S(1)}, u32[]{:S(2)}, u32[]{:S(2)}) collective-permute-start(f32[48,128]{1,0:T(8,128)} %get-tuple-element.16.refs_0_), channel_id=1, source_target_pairs={{0,3},{1,0},{2,1},{3,2},{4,7},{5,4},{6,5},{7,6},{8,11},{9,8},{10,9... | collective-permute-start | bytes 73736 | tf_op jit(solution)/shard_map/ppermute | solution.py:325
  13.4 0.6 %collective-permute-start.1 = (f32[48,128]{1,0:T(8,128)}, f32[48,128]{1,0:T(8,128)S(1)}, u32[]{:S(2)}, u32[]{:S(2)}) collective-permute-start(f32[48,128]{1,0:T(8,128)} %get-tuple-element.16.refs_0_), channel_id=1, source_target_pairs={{0,2},{1,3},{2,0},{3,1},{4,6},{5,7},{6,4},{7,5},{8,10},{9,11},{10,... | collective-permute-start | bytes 73736 | tf_op jit(solution)/shard_map/ppermute | solution.py:325
  14.0 0.2 collective-permute-start
  14.1 0.9 %collective-permute-done.2.refs_3_ = f32[48,128]{1,0:T(8,128)S(1)} collective-permute-done((f32[48,128]{1,0:T(8,128)}, f32[48,128]{1,0:T(8,128)S(1)}, u32[]{:S(2)}, u32[]{:S(2)}) %collective-permute-start.2) | collective-permute-done | bytes 24608 | tf_op jit(solution)/shard_map/ppermute | solution.py:325
  15.1 0.0 copy-start.1
  15.1 2.5 %collective-permute-done.1.refs_2_ = f32[48,128]{1,0:T(8,128)S(1)} collective-permute-done((f32[48,128]{1,0:T(8,128)}, f32[48,128]{1,0:T(8,128)S(1)}, u32[]{:S(2)}, u32[]{:S(2)}) %collective-permute-start.1) | collective-permute-done | bytes 24608 | tf_op jit(solution)/shard_map/ppermute | solution.py:325
  17.6 0.0 copy-start.2
  17.6 0.1 collective-permute-done.refs_1_
  17.7 0.0 copy-done.1
  17.7 0.5 %copy-done.2 = f32[48,128]{1,0:T(8,128)} copy-done((f32[48,128]{1,0:T(8,128)}, f32[48,128]{1,0:T(8,128)S(1)}, u32[]{:S(2)}) %copy-start.2) | copy-done | bytes 24600
  18.2 0.0 copy-start.3
  18.2 0.6 %copy-done.3 = f32[48,128]{1,0:T(8,128)} copy-done((f32[48,128]{1,0:T(8,128)}, f32[48,128]{1,0:T(8,128)S(1)}, u32[]{:S(2)}) %copy-start.3) | copy-done | bytes 24600
  18.8 1.4 %shard_map.148 = (f32[32,128]{1,0:T(8,128)}, f32[8,16,128]{2,1,0:T(8,128)}) custom-call(f32[48,128]{1,0:T(8,128)} %get-tuple-element.16.refs_0_, f32[48,128]{1,0:T(8,128)} %copy-done.3, f32[48,128]{1,0:T(8,128)} %copy-done.2, f32[48,128]{1,0:T(8,128)} %copy-done.1), custom_call_target="tpu_custom_call" | custom-call | tf_op jit(solution)/shard_map/pallas_call | solution.py:327
  20.2 5.8 %all-to-all-start = ((f32[8,16,128]{2,1,0:T(8,128)}), f32[8,16,128]{2,1,0:T(8,128)S(1)}, u32[]{:S(2)}, u32[]{:S(2)}) async-start(f32[8,16,128]{2,1,0:T(8,128)} %get-tuple-element.18), calls=%async_computation | async-start | bytes 131072 | tf_op jit(solution)/shard_map/all_to_all | solution.py:334
  26.1 4.9 %shard_map.147 = bf16[64,8192]{1,0:T(8,128)(2,1)} custom-call(s32[1]{0:T(128)S(6)} %copy.16.live_ref, bf16[64,256]{1,0:T(8,128)(2,1)} %ns_ref.3, bf16[272,144]{1,0:T(8,128)(2,1)} %get-tuple-element.14.table_ref, f32[256,128]{1,0:T(8,128)} %get-tuple-element.15.weight_ref, bf16[64,8192]{1,0:T(8,128)(2,1)} %sec_ref.3, bf16[64,8192]{1,0:T(8,128)(2,1)} %mst_ref.3, ...), custom_call_target="tpu_custom_call" | custom-call | flops 17448304640 | bytes 3145728 | tf_op jit(solution)/shard_map/pallas_call | solution.py:237
  31.0 2.0 %all-to-all-done.arrived_ref = f32[8,16,128]{2,1,0:T(8,128)S(1)} async-done(((f32[8,16,128]{2,1,0:T(8,128)}), f32[8,16,128]{2,1,0:T(8,128)S(1)}, u32[]{:S(2)}, u32[]{:S(2)}) %all-to-all-start) | async-done | bytes 65568 | tf_op jit(solution)/shard_map/all_to_all | solution.py:334
  33.0 0.0 copy-start
  33.0 0.6 %copy-done = f32[8,16,128]{2,1,0:T(8,128)} copy-done((f32[8,16,128]{2,1,0:T(8,128)}, f32[8,16,128]{2,1,0:T(8,128)S(1)}, u32[]{:S(2)}) %copy-start) | copy-done | bytes 65560
  33.6 1.5 %shard_map.149 = (f32[8,128]{1,0:T(8,128)}, s32[8,128]{1,0:T(8,128)}, f32[8,128]{1,0:T(8,128)}, f32[1,1]{1,0:T(1,128)}) custom-call(s32[1]{0:T(128)} %bitcast.6.before_ref, f32[32,128]{1,0:T(8,128)} %get-tuple-element.17.own_ref, f32[8,16,128]{2,1,0:T(8,128)} %copy-done), custom_call_target="tpu_custom_call" | custom-call | tf_op jit(solution)/shard_map/pallas_call | solution.py:339
Async XLA Ops:
  10.9 4.1 %collective-permute-start.2 = (f32[48,128]{1,0:T(8,128)}, f32[48,128]{1,0:T(8,128)S(1)}, u32[]{:S(2)}, u32[]{:S(2)}) collective-permute-start(f32[48,128]{1,0:T(8,128)} %get-tuple-element.16.refs_0_), channel_id=1, source_target_pairs={{0,3},{1,0},{2,1},{3,2},{4,7},{5,4},{6,5},{7,6},{8,11},{9,8},{10,9... | collective-permute-start | bytes 73736 | tf_op jit(solution)/shard_map/ppermute | solution.py:325
  13.4 4.2 %collective-permute-start.1 = (f32[48,128]{1,0:T(8,128)}, f32[48,128]{1,0:T(8,128)S(1)}, u32[]{:S(2)}, u32[]{:S(2)}) collective-permute-start(f32[48,128]{1,0:T(8,128)} %get-tuple-element.16.refs_0_), channel_id=1, source_target_pairs={{0,2},{1,3},{2,0},{3,1},{4,6},{5,7},{6,4},{7,5},{8,10},{9,11},{10,... | collective-permute-start | bytes 73736 | tf_op jit(solution)/shard_map/ppermute | solution.py:325
  14.0 3.7 %collective-permute-start = (f32[48,128]{1,0:T(8,128)}, f32[48,128]{1,0:T(8,128)S(1)}, u32[]{:S(2)}, u32[]{:S(2)}) collective-permute-start(f32[48,128]{1,0:T(8,128)} %get-tuple-element.16.refs_0_), channel_id=1, source_target_pairs={{0,1},{1,2},{2,3},{3,0},{4,5},{5,6},{6,7},{7,4},{8,9},{9,10},{10,1... | collective-permute-start | bytes 73736 | tf_op jit(solution)/shard_map/ppermute | solution.py:325
  15.1 2.6 %copy-start.1 = (f32[48,128]{1,0:T(8,128)}, f32[48,128]{1,0:T(8,128)S(1)}, u32[]{:S(2)}) copy-start(f32[48,128]{1,0:T(8,128)S(1)} %collective-permute-done.2.refs_3_) | copy-start | bytes 73732
  17.6 0.6 %copy-start.2 = (f32[48,128]{1,0:T(8,128)}, f32[48,128]{1,0:T(8,128)S(1)}, u32[]{:S(2)}) copy-start(f32[48,128]{1,0:T(8,128)S(1)} %collective-permute-done.1.refs_2_) | copy-start | bytes 73732
  18.2 0.6 %copy-start.3 = (f32[48,128]{1,0:T(8,128)}, f32[48,128]{1,0:T(8,128)S(1)}, u32[]{:S(2)}) copy-start(f32[48,128]{1,0:T(8,128)S(1)} %collective-permute-done.refs_1_) | copy-start | bytes 73732
  20.2 12.7 %all-to-all-start = ((f32[8,16,128]{2,1,0:T(8,128)}), f32[8,16,128]{2,1,0:T(8,128)S(1)}, u32[]{:S(2)}, u32[]{:S(2)}) async-start(f32[8,16,128]{2,1,0:T(8,128)} %get-tuple-element.18), calls=%async_computation | async-start | bytes 131072 | tf_op jit(solution)/shard_map/all_to_all | solution.py:334
  33.0 0.6 %copy-start = (f32[8,16,128]{2,1,0:T(8,128)}, f32[8,16,128]{2,1,0:T(8,128)S(1)}, u32[]{:S(2)}) copy-start(f32[8,16,128]{2,1,0:T(8,128)S(1)} %all-to-all-done.arrived_ref) | copy-start | bytes 196612
